TPU v7x, 256 devices: a 4x2x16 block of a 4x16x16 slice. The times are simulated.
256 devices in a mesh: groups: 2 (over y), dp: 32 (over z, core), mp: 4 (over x).
Axes of the slice: x: 4, y: 2, z: 16, core: 2. Of those that a mesh axis runs over, the one named last changes fastest.
The devices are a block of a 4x16x16 slice.
Arguments:
- tokens: bfloat16 [8192, 7168], P(('groups', 'dp')), parts along dimension 0, may hold values from -20 to 20, as said below
- w_down: bfloat16 [7168, 1536], P('dp', 'mp'), may hold values from -3 to 3, as said below
- gain: float32 [1536], P('mp'), may hold values from 0.25 to 1.75
- w_up: bfloat16 [1536, 26112], P('dp', 'mp'), may hold values from -0.15625 to 0.15625
- head_counts: int32 [4], replicated, may hold values from 30 to 34, as said below
- cotangent: bfloat16 [8192, 26112], P(('groups', 'dp'), 'mp'), parts along dimension 0, may hold values from -6 to 6
Outputs:
- queries: bfloat16 [8192, 26112], P(('groups', 'dp'), 'mp'), parts along dimension 0
- grad_tokens: bfloat16 [8192, 7168], P(('groups', 'dp'), 'mp'), parts along dimension 0
There are 2 independent parts, one for each index of `groups`. A program takes and returns all parts, laid end to end along the dimension named above; an argument that names none is the same for every part. Nothing has to cross between parts.
Inputs may be any that keep to these rules, and one draw needn't show every extreme that they name: `tokens`: hidden states of order one with token scales that differ. `w_down`: entries of order 7168^(-1/2). `head_counts`: the entries sum to 128; one of them is 34.
All inputs are finite; a program needn't handle non-finite values.
Results may differ from a plain program's by a relative error of at most 0.018.
Values may be sent and summed in bfloat16 or wider, within the bound.
A program may use at most 128 MiB of HBM per device.

v0:
```python
import jax
import jax.numpy as jnp
from jax import lax
from jax.sharding import PartitionSpec as P

HD = 192


def laid_out(blocks, dim):
    shape = list(blocks.shape[1:])
    shape[dim] *= blocks.shape[0]
    return jnp.moveaxis(blocks, 0, dim).reshape(shape)


def from_everyone(array, axis):
    size = lax.axis_size(axis)
    return lax.all_to_all(
        jnp.broadcast_to(array[None], (size, *array.shape)), axis, 0, 0, tiled=True
    )


def gather_directly(array, axis, dim):
    return laid_out(from_everyone(array, axis), dim)


def cut_along(array, dim, size):
    shape = array.shape
    blocks = array.reshape(*shape[:dim], size, shape[dim] // size, *shape[dim + 1 :])
    return jnp.moveaxis(blocks, dim, 0)


def sent_and_summed(array, axis, dim):
    size = lax.axis_size(axis)
    blocks = lax.all_to_all(cut_along(array, dim, size), axis, 0, 0, tiled=True)
    return jnp.sum(blocks.astype(jnp.float32), axis=0)


def contract_last(left, right):
    return lax.dot_general(
        left, right, (((1,), (1,)), ((), ())), preferred_element_type=jnp.float32
    )


def body(tokens, w_down, gain, w_up, head_counts, cotangent):
    block_cols = w_up.shape[1]
    latent_width = w_down.shape[1] * lax.axis_size("mp")
    position = lax.axis_index("mp")
    held_heads = lax.dynamic_slice_in_dim(head_counts, position, 1, 0)
    slot_index = jnp.arange(block_cols, dtype=jnp.int32) // HD
    keep_mask = (slot_index < held_heads).astype(jnp.float32)
    down_whole = lax.all_gather(w_down, "dp", axis=0, tiled=True)
    latent_raw = jnp.dot(tokens, down_whole, preferred_element_type=jnp.float32)
    squares = lax.psum(jnp.sum(latent_raw * latent_raw, axis=1, keepdims=True), "mp")
    root_mean = jnp.sqrt(squares / latent_width + 1e-06)
    latent_local = (latent_raw / root_mean * gain).astype(jnp.bfloat16)
    latent = gather_directly(latent_local, "mp", 1)
    masked = cotangent * keep_mask.astype(jnp.bfloat16)
    up_whole = lax.all_gather(w_up, "dp", axis=0, tiled=True)
    query_total = jnp.dot(latent, up_whole, preferred_element_type=jnp.float32)
    grad_partial = contract_last(masked, up_whole)
    queries = (query_total * keep_mask).astype(jnp.bfloat16)
    grad_latent = sent_and_summed(grad_partial.astype(jnp.bfloat16), "mp", 1)
    inner_dot = lax.psum(jnp.sum(gain * grad_latent * latent_raw, axis=1, keepdims=True), "mp")
    grad_raw = (
        gain * grad_latent / root_mean - latent_raw * inner_dot / (latent_width * root_mean**3)
    ).astype(jnp.bfloat16)
    partial_value = contract_last(grad_raw, down_whole).astype(jnp.bfloat16).astype(jnp.float32)
    grad_tokens = sent_and_summed(partial_value.astype(jnp.bfloat16), "mp", 1).astype(jnp.bfloat16)
    return (queries, grad_tokens)


def solution(mesh):
    in_specs = (
        P(("groups", "dp"), None),
        P("dp", "mp"),
        P("mp"),
        P("dp", "mp"),
        P(),
        P(("groups", "dp"), "mp"),
    )
    out_specs = (P(("groups", "dp"), "mp"), P(("groups", "dp"), "mp"))
    return jax.shard_map(body, mesh=mesh, in_specs=in_specs, out_specs=out_specs, check_vma=False)
```

profile of v0, /device:TPU:33, one launch (start us, length us, event | category | flops | bytes accessed | tf_op | source)
XLA Modules:
  0.0 276.7 jit_solution(305809374449515332)
XLA Ops:
  7.2 0.0 copy-start
  7.2 0.1 all-gather.5.cloned.1.call-start
  7.3 0.7 all-gather.5.cloned.1.call-update
  8.0 0.1 all-gather.3.cloned.1.call-start
  8.1 0.7 all-gather.3.cloned.1.call-update
  8.8 1.2 dynamic_slice.3
  10.0 0.7 fusion.12
  10.7 0.0 copy-start.1
  10.7 135.5 %all-gather.5.cloned.1.call-done = bf16[1536,6528]{1,0:T(8,128)(2,1)} async-done(((bf16[48,6528]{1,0:T(8,128)(2,1)}), bf16[1536,6528]{1,0:T(8,128)(2,1)}) %all-gather.5.cloned.1.call-update) | async-done | bytes 20054032 | tf_op jit(solution)/shard_map/all_gather | solution.py:58
  146.3 10.2 %convolution_convert_fusion.1 = bf16[128,1536]{1,0:T(8,128)(2,1)S(1)} fusion(bf16[1536,6528]{1,0:T(8,128)(2,1)} %all-gather.5.cloned.1.call-done, bf16[128,6528]{1,0:T(8,128)(2,1)} %param.11, bf16[6528]{0:T(1024)(128)(2,1)S(1)} %fusion.12), kind=kOutput, calls=%fused_computation.3 | convolution fusion | flops 2567946240 | bytes 22131456 | tf_op jit(solution)/shard_map/dot_general | solution.py:39
  156.5 11.4 %all_to_all.15 = bf16[4,128,384]{2,1,0:T(8,128)(2,1)S(1)} all-to-all(bf16[4,128,384]{2,1,0:T(8,128)(2,1)S(1)} %bitcast.33), channel_id=1, replica_groups=mesh['groups'=2,'dp'=32,'mp'=4] {'mp'}, dimensions={0} | all-to-all | bytes 786432 | tf_op jit(solution)/shard_map/all_to_all | solution.py:34
  168.0 51.6 %all-gather.3.cloned.1.call-done = bf16[7168,384]{1,0:T(8,128)(2,1)} async-done(((bf16[224,384]{1,0:T(8,128)(2,1)}), bf16[7168,384]{1,0:T(8,128)(2,1)}) %all-gather.3.cloned.1.call-update) | async-done | bytes 5505040 | tf_op jit(solution)/shard_map/all_gather | solution.py:51
  219.6 0.0 copy-done
  219.6 0.0 copy-done.1
  219.6 3.8 %multiply_reduce_fusion = (f32[128]{0:T(128)S(1)}, f32[128]{0:T(128)S(1)}, f32[128,384]{1,0:T(8,128)S(1)}) fusion(f32[128,384]{1,0:T(8,128)S(1)} %convert_reduce_fusion, f32[384]{0:T(512)S(1)} %copy-done.1, bf16[128,7168]{1,0:T(8,128)(2,1)S(1)} %copy-done, bf16[7168,384]{1,0:T(8,128)(2,1)} %all-gather.3.cloned.1.call-done), kind=kOutput, calls=%fused_computation.10 | convolution fusion | flops 704888576 | bytes 7735808 | tf_op jit(solution)/shard_map/dot_general | solution.py:52
  223.4 8.4 %all-reduce = (f32[128,1]{0,1:T(1,128)S(1)}, f32[128]{0:T(128)S(1)}) all-reduce(f32[128,1]{0,1:T(1,128)S(1)} %bitcast.34, f32[128]{0:T(128)S(1)} %get-tuple-element.2), channel_id=1, replica_groups=mesh['groups'=2,'dp'=32,'mp'=4] {'mp'}, use_global_device_ids=true, to_apply=%region_1.2 | all-reduce | flops 256 | bytes 2048 | tf_op jit(solution)/shard_map/psum | solution.py:53
  231.8 0.1 multiply_convert_fusion
  231.9 0.1 copy.9
  232.1 0.8 broadcast_in_dim.7
  232.9 3.6 %all-to-all-start = ((bf16[4,128,384]{1,2,0:T(8,128)(2,1)}), bf16[4,128,384]{1,2,0:T(8,128)(2,1)S(1)}, u32[]{:S(2)}, u32[]{:S(2)}) async-start(bf16[4,128,384]{1,2,0:T(8,128)(2,1)} %broadcast_in_dim.7), calls=%async_computation | async-start | bytes 786432 | tf_op jit(solution)/shard_map/all_to_all | solution.py:17
  236.4 4.4 %convolution_convert_fusion = bf16[128,7168]{1,0:T(8,128)(2,1)S(1)} fusion(bf16[7168,384]{1,0:T(8,128)(2,1)} %all-gather.3.cloned.1.call-done, f32[128,384]{1,0:T(8,128)S(1)} %get-tuple-element.8, f32[128,384]{1,0:T(8,128)S(1)} %convert_reduce_fusion, f32[128]{0:T(128)S(1)} %get-tuple-element.6, f32[128]{0:T(128)S(1)} %get-tuple-element.5, ...), kind=kOutput, calls=%fused_computation.2 | convolution fusion | flops 705855488 | bytes 7736320 | tf_op jit(solution)/shard_map/dot_general | solution.py:39
  240.8 1.4 copy.16
  242.3 0.3 all-to-all-done
  242.6 4.5 %all-to-all-start.2 = ((bf16[4,128,1792]{2,1,0:T(8,128)(2,1)}), bf16[4,128,1792]{2,1,0:T(8,128)(2,1)}, u32[]{:S(2)}, u32[]{:S(2)}) async-start(bf16[4,128,1792]{2,1,0:T(8,128)(2,1)} %bitcast.29), calls=%async_computation.2 | async-start | bytes 3670016 | tf_op jit(solution)/shard_map/all_to_all | solution.py:34
  247.1 0.7 fusion.10
  247.7 10.9 %fusion = bf16[128,6528]{1,0:T(8,128)(2,1)} fusion(bf16[128,1536]{0,1:T(8,128)(2,1)S(1)} %bitcast.31, bf16[1536,6528]{1,0:T(8,128)(2,1)} %all-gather.5.cloned.1.call-done, f32[6528]{0:T(1024)S(1)} %fusion.10), kind=kOutput, calls=%fused_computation.1 | convolution fusion | flops 2568585216 | bytes 22144512 | tf_op jit(solution)/shard_map/dot_general | solution.py:59
  258.6 8.6 %all-to-all-done.2 = bf16[4,128,1792]{2,1,0:T(8,128)(2,1)} async-done(((bf16[4,128,1792]{2,1,0:T(8,128)(2,1)}), bf16[4,128,1792]{2,1,0:T(8,128)(2,1)}, u32[]{:S(2)}, u32[]{:S(2)}) %all-to-all-start.2) | async-done | bytes 1835040 | tf_op jit(solution)/shard_map/all_to_all | solution.py:34
  267.2 2.7 reduce_sum.42
  (3 shorter events, 0.1 us)
Async XLA Ops:
  7.2 212.4 %copy-start = (bf16[128,7168]{1,0:T(8,128)(2,1)S(1)}, bf16[128,7168]{1,0:T(8,128)(2,1)}, u32[]{:S(2)}) copy-start(bf16[128,7168]{1,0:T(8,128)(2,1)} %param.6) | copy-start | bytes 5505028
  7.2 139.1 %all-gather.5.cloned.1.call-start = ((), (), s32[]{:S(2)}) async-start(), calls=%async_computation.4 | async-start | bytes 20680704 | tf_op jit(solution)/shard_map/all_gather | solution.py:58
  8.0 211.6 %all-gather.3.cloned.1.call-start = ((), (), s32[]{:S(2)}) async-start(), calls=%async_computation.3 | async-start | bytes 5677056 | tf_op jit(solution)/shard_map/all_gather | solution.py:51
  10.7 208.9 %copy-start.1 = (f32[384]{0:T(512)S(1)}, f32[384]{0:T(512)}, u32[]{:S(2)}) copy-start(f32[384]{0:T(512)} %param.8) | copy-start | bytes 4612
  232.9 9.7 %all-to-all-start = ((bf16[4,128,384]{1,2,0:T(8,128)(2,1)}), bf16[4,128,384]{1,2,0:T(8,128)(2,1)S(1)}, u32[]{:S(2)}, u32[]{:S(2)}) async-start(bf16[4,128,384]{1,2,0:T(8,128)(2,1)} %broadcast_in_dim.7), calls=%async_computation | async-start | bytes 786432 | tf_op jit(solution)/shard_map/all_to_all | solution.py:17
  242.6 24.6 %all-to-all-start.2 = ((bf16[4,128,1792]{2,1,0:T(8,128)(2,1)}), bf16[4,128,1792]{2,1,0:T(8,128)(2,1)}, u32[]{:S(2)}, u32[]{:S(2)}) async-start(bf16[4,128,1792]{2,1,0:T(8,128)(2,1)} %bitcast.29), calls=%async_computation.2 | async-start | bytes 3670016 | tf_op jit(solution)/shard_map/all_to_all | solution.py:34
Sparse Core Ops, SparseCore 0:
  9.9 136.3 all-gather.4
  148.1 71.4 all-gather.2
where the time goes:
time: 279 us; the launch traced here: 277 us
  waiting for transfers between devices  198 us (71%)
  matrix products  29.2 us (10%)
  blocking collectives  19.8 us (7%)
  between operations  14.2 us (5%)
  starting transfers between devices  8.15 us (3%)
  other arithmetic  4.13 us (1%)
  local copies, waits for them, and re-layouts  3.65 us (1%)
    all_gather x1, waiting for transfers between devices, body(): up_whole = lax.all_gather(w_up, 'dp', axis=0, tiled=True)  136 us
    all_gather x1, waiting for transfers between devices, body(): down_whole = lax.all_gather(w_down, 'dp', axis=0, tiled=True)  51.6 us
    dot_general x2, matrix products, contract_last(): lax.dot_general(left, right, (((1,), (1,)), ((), ())), preferred_element_...  14.6 us
    all_to_all x1, blocking collectives, sent_and_summed(): blocks = lax.all_to_all(cut_along(array, dim, size), axis, 0, 0, tiled=True)  11.4 us
    dot_general x1, matrix products, body(): query_total = jnp.dot(latent, up_whole, preferred_element_type=jnp.float32)  10.9 us
    all_to_all x1, waiting for transfers between devices, sent_and_summed(): blocks = lax.all_to_all(cut_along(array, dim, size), axis, 0, 0, tiled=True)  8.65 us
    psum x1, blocking collectives, body(): lax.psum(jnp.sum(latent_raw * latent_raw, axis=1, keepdims=True), 'mp')  8.44 us
  transfers between devices with their start and end apart: 4, of which 4 were waited for; matrix products, arithmetic and copies ran while one was open for 11% of the time, Pallas kernels for 0%

commit v1 on v0

v1 whole, which is shorter than its diff:
```python
import functools

import jax
import jax.numpy as jnp
from jax import lax
from jax.experimental import pallas as pl
from jax.experimental.pallas import tpu as pltpu
from jax.sharding import PartitionSpec as P

HD = 192
MESH = pl.DeviceIdType.MESH
F32 = jnp.float32
BF16 = jnp.bfloat16
CHUNK = 384


def kernel(
    tok_h, wd_h, gain_ref, wu_h, heads_ref, cot_h, q_h, gt_h,
    tok, wd, wd2, wu, cot, cot_t, lr_t, lat_t, gain_b, gain_all,
    own_gl, send_gl, peer_gl, grad_raw, q_acc, q_out, gt_out, root,
    load_sem, out_sem, z_send, z_recv, y_send, c_send, c_recv,
    lr_send, lr_recv, ga_send, ga_recv, w2_send, w2_recv, w2c_send, w2c_recv, gl_send, gl_recv,
):
    n_dp, n_mp = lax.axis_size("dp"), lax.axis_size("mp")
    n_z = n_dp // 2
    half = n_z // 2
    me_g, me_dp, me_x = lax.axis_index("groups"), lax.axis_index("dp"), lax.axis_index("mp")
    z, core = me_dp // 2, me_dp % 2
    plane = me_g % 2
    partner = me_g + 1 - 2 * plane
    after, before = (me_dp + 2) % n_dp, (me_dp + n_dp - 2) % n_dp
    sibling = me_dp + 1 - 2 * core

    up_rows, cols = wu_h.shape
    down_rows, lat_cols = wd_h.shape
    n_tok, width = tok_h.shape
    lat = lat_cols * n_mp
    out_cols = width // n_mp
    rows3, cols3 = up_rows // 3, lat_cols // 3
    part_a, part_b, part_c = 2 * plane, 1, 2 * (1 - plane)

    def block(kind, bz, bc):
        if kind == 0:
            return wd.at[pl.ds(pl.multiple_of((2 * bz + bc) * down_rows, down_rows), down_rows), :]
        return wu.at[pl.ds(pl.multiple_of((2 * bz + bc) * up_rows, up_rows), up_rows), :]

    def piece(kind, bz, part):
        if kind == 0:
            rows = pl.ds(pl.multiple_of((2 * bz + core) * down_rows, down_rows), down_rows)
            return wd.at[rows, pl.ds(pl.multiple_of(part * cols3, cols3), cols3)]
        return wu.at[pl.ds(pl.multiple_of((2 * bz + core) * up_rows + part * rows3, rows3), rows3), :]

    def remote(src, dst, send, recv, where):
        return pltpu.make_async_remote_copy(
            src_ref=src, dst_ref=dst, send_sem=send, recv_sem=recv, device_id=where, device_id_type=MESH
        )

    def z_copy(kind, way, bz, part):
        ref = piece(kind, bz, part)
        return remote(
            ref, ref, z_send.at[kind, way, part, bz], z_recv.at[kind, part, bz], {"dp": (after, before)[way]}
        )

    def y_copy(kind, bz, part):
        ref = piece(kind, bz, part)
        return remote(ref, ref, y_send.at[kind, bz], z_recv.at[kind, part, bz], {"groups": partner})

    def c_copy(kind, bz, bc):
        ref = block(kind, bz, bc)
        return remote(ref, ref, c_send.at[kind, bz], c_recv.at[kind, bz], {"dp": sibling})

    def left(s):
        return (z + n_z - s) % n_z

    def right(s):
        return (z + s) % n_z

    own_down = pltpu.make_async_copy(wd_h, block(0, z, core), load_sem.at[0])
    own_up = pltpu.make_async_copy(wu_h, block(1, z, core), load_sem.at[1])
    load_cot = pltpu.make_async_copy(cot_h, cot, load_sem.at[2])
    load_tok = pltpu.make_async_copy(tok_h, tok, load_sem.at[3])
    own_down.start()
    own_up.start()
    load_cot.start()
    load_tok.start()

    barrier = pltpu.get_barrier_semaphore()
    others = [{"dp": after}, {"dp": before}, {"dp": sibling}, {"groups": partner}]
    others += [{"mp": (me_x + i) % n_mp} for i in range(1, n_mp)]
    for where in others:
        pl.semaphore_signal(barrier, inc=1, device_id=where, device_id_type=MESH)
    pl.semaphore_wait(barrier, len(others))

    def send_own(kind):
        for part in (part_a, part_b):
            for way in (0, 1):
                z_copy(kind, way, z, part).start()
        c_copy(kind, z, core).start()

    def ring_step(kind, s):
        lz, rz = left(s), right(s)
        z_copy(kind, 0, lz, part_a).wait_recv()
        z_copy(kind, 0, lz, part_a).start()
        y_copy(kind, lz, part_a).start()
        z_copy(kind, 1, rz, part_a).wait_recv()

        @pl.when(s < half - 1)
        def _():
            z_copy(kind, 1, rz, part_a).start()

        y_copy(kind, rz, part_a).start()
        z_copy(kind, 0, lz, part_b).wait_recv()

        @pl.when(s < half - 1)
        def _():
            z_copy(kind, 0, lz, part_b).start()

        z_copy(kind, 1, rz, part_b).wait_recv()
        z_copy(kind, 1, rz, part_b).start()

    def last_step(kind):
        far = right(half)
        z_copy(kind, 0, far, part_a).wait_recv()
        y_copy(kind, far, part_a).start()
        z_copy(kind, 1, far, part_b).wait_recv()

    def share(kind, bz):
        y_copy(kind, bz, part_c).wait_recv()
        c_copy(kind, bz, core).start()

    def share_pair(kind, s):
        share(kind, left(s))
        share(kind, right(s))

    def wait_sibling(kind, bz):
        c_copy(kind, bz, 1 - core).wait_recv()

    held = jnp.int32(0)
    for i in range(n_mp):
        held = held + jnp.where(me_x == i, heads_ref[i], 0)
    kept = held * HD
    lane = lax.broadcasted_iota(jnp.int32, (1, CHUNK), 1)
    lane1 = lax.broadcasted_iota(jnp.int32, (1, 128), 1)

    own_down.wait()
    send_own(0)
    own_up.wait()
    x_peers = [((me_x + i) % n_mp, (me_x + n_mp - i) % n_mp) for i in range(1, n_mp)]

    def gain_copy(i):
        return remote(
            gain_all.at[me_x], gain_all.at[me_x], ga_send.at[i], ga_recv.at[i], {"mp": x_peers[i][0]}
        )

    gain_all[me_x] = gain_ref[...]
    load_cot.wait()
    n_blocks = cols // 128
    per_step = -(-n_blocks // (half - 1))

    def turn(j, _):
        at = pl.ds(pl.multiple_of(j * 128, 128), 128)
        value = jnp.where(lane1 + j * 128 < kept, cot[:, at], jnp.zeros((), BF16))
        cot_t[at, :] = value.T
        return 0

    def down_step(s, _):
        ring_step(0, s)
        lax.fori_loop((s - 1) * per_step, jnp.minimum(s * per_step, n_blocks), turn, 0)
        return 0

    lax.fori_loop(1, half, down_step, 0)
    send_own(1)
    for i in range(n_mp - 1):
        gain_copy(i).start()
    last_step(0)

    def share_down(s, _):
        share_pair(0, s)
        return 0

    lax.fori_loop(1, half, share_down, 0)
    share(0, right(half))
    load_tok.wait()

    def wait_down(bz, _):
        wait_sibling(0, bz)
        return 0

    lax.fori_loop(0, n_z, wait_down, 0)

    k_size = width // 7

    def latent_part(k, total):
        at = pl.ds(pl.multiple_of(k * k_size, k_size), k_size)
        return total + jnp.dot(tok[:, at], wd[at, :], preferred_element_type=F32)

    latent_raw = lax.fori_loop(0, 7, latent_part, jnp.zeros((n_tok, lat_cols), F32))

    def lat_rows(owner):
        return pl.ds(pl.multiple_of(owner * lat_cols, lat_cols), lat_cols)

    lr_t[lat_rows(me_x), :] = latent_raw.T

    def lr_copy(i, owner):
        ref = lr_t.at[lat_rows(owner), :]
        return remote(ref, ref, lr_send.at[i], lr_recv.at[i], {"mp": x_peers[i][0]})

    half_out = out_cols // 2

    def w2_copy(i):
        to, came_from = x_peers[i]
        rows = pl.ds(pl.multiple_of(to * out_cols + core * half_out, half_out), half_out)
        mine = pl.ds(pl.multiple_of(core * half_out, half_out), half_out)
        return remote(wd.at[rows, :], wd2.at[me_x, mine, :], w2_send.at[i], w2_recv.at[i], {"mp": to})

    def w2_arrived(i, bc):
        rows = pl.ds(pl.multiple_of(bc * half_out, half_out), half_out)
        return wd2.at[x_peers[i][1], rows, :]

    def w2_share(i, bc):
        ref = w2_arrived(i, bc)
        return remote(ref, ref, w2c_send.at[i], w2c_recv.at[i], {"dp": sibling})

    for i in range(n_mp - 1):
        lr_copy(i, me_x).start()
    for i in range(n_mp - 1):
        w2_copy(i).start()
    r_size = out_cols // 7

    def own_part(k, _):
        to = pl.ds(pl.multiple_of(k * r_size, r_size), r_size)
        came = pl.ds(pl.multiple_of(me_x * out_cols + k * r_size, r_size), r_size)
        wd2[me_x, to, :] = wd[came, :]
        return 0

    lax.fori_loop(0, 7, own_part, 0)

    ring_step(1, 1)

    for i in range(n_mp - 1):
        ref = gain_all.at[x_peers[i][1]]
        remote(ref, ref, ga_send.at[i], ga_recv.at[i], {"mp": x_peers[i][0]}).wait_recv()
    for b in range(n_mp):
        gain_b[b * lat_cols : (b + 1) * lat_cols, :] = jnp.broadcast_to(gain_all[b], (n_tok, lat_cols)).T
    for i in range(n_mp - 1):
        lr_copy(i, x_peers[i][1]).wait_recv()
    squares = jnp.zeros((1, n_tok), F32)
    for b in range(n_mp):
        value = lr_t[b * lat_cols : (b + 1) * lat_cols, :]
        squares = squares + jnp.sum(value * value, axis=0, keepdims=True)
    root[...] = jnp.sqrt(squares / lat + 1e-06)
    for b in range(n_mp):
        at = slice(b * lat_cols, (b + 1) * lat_cols)
        lat_t[at, :] = (lr_t[at, :] / root[...] * gain_b[at, :]).astype(BF16)

    z_rows = 2 * up_rows

    def rows_of(bz):
        return pl.ds(pl.multiple_of(bz * z_rows, z_rows), z_rows)

    def gl_copy(i, bz):
        return remote(
            send_gl.at[rows_of(bz), :], peer_gl.at[i, rows_of(bz), :],
            gl_send.at[i, bz], gl_recv.at[i, bz], {"mp": x_peers[i][0]},
        )

    def publish(bz, value):
        own_gl[rows_of(bz), :] = value
        send_gl[rows_of(bz), :] = value.astype(BF16)

    def send_blocks(zs):
        for bz in zs:
            for i in range(n_mp - 1):
                gl_copy(i, bz).start()

    def chunk_at(c):
        return pl.ds(pl.multiple_of(c * CHUNK, CHUNK), CHUNK)

    n_chunks = cols // CHUNK

    def compute(zs, gl=True, q=True, first=False, final=False):
        lefts = [lat_t[rows_of(bz), :].T for bz in zs] if q else None

        def step(c, totals):
            at = chunk_at(c)
            tiles = [wu[rows_of(bz), at] for bz in zs]
            if q:
                value = jnp.dot(lefts[0], tiles[0], preferred_element_type=F32)
                for one, tile in zip(lefts[1:], tiles[1:]):
                    value = value + jnp.dot(one, tile, preferred_element_type=F32)
                if not first:
                    value = value + q_acc[:, at]
                if final:
                    q_out[:, at] = jnp.where(lane + c * CHUNK < kept, value, 0.0).astype(BF16)
                else:
                    q_acc[:, at] = value
            if gl:
                side = cot_t[at, :]
                totals = tuple(
                    total + jnp.dot(tile, side, preferred_element_type=F32) for total, tile in zip(totals, tiles)
                )
            return totals

        start = tuple(jnp.zeros((z_rows, n_tok), F32) for _ in zs) if gl else ()
        totals = lax.fori_loop(0, n_chunks, step, start)
        if gl:
            for bz, total in zip(zs, totals):
                publish(bz, total)
            send_blocks(zs)

    ring_step(1, 2)
    share_pair(1, 1)
    wait_sibling(1, z)
    compute([z], first=True)

    def up_step(s, _):
        ring_step(1, s)
        share_pair(1, s - 1)
        zs = [left(s - 2), right(s - 2)]
        for bz in zs:
            wait_sibling(1, bz)
        compute(zs)
        return 0

    lax.fori_loop(3, half, up_step, 0)
    last_step(1)
    share_pair(1, half - 1)
    zs = [left(half - 2), right(half - 2)]
    for bz in zs:
        wait_sibling(1, bz)
    compute(zs)
    far = right(half)
    share(1, far)
    zs = [left(half - 1), right(half - 1)]
    for bz in zs:
        wait_sibling(1, bz)
    compute(zs)
    for i in range(n_mp - 1):
        ref = w2_arrived(i, core)
        remote(ref, ref, w2_send.at[i], w2_recv.at[i], {"mp": x_peers[i][0]}).wait_recv()
        w2_share(i, core).start()
    wait_sibling(1, far)
    compute([far], q=False)
    compute([far], gl=False, final=True)
    q_store = pltpu.make_async_copy(q_out, q_h, out_sem.at[0])
    q_store.start()

    def wait_gl(bz, _):
        for i in range(n_mp - 1):
            gl_copy(i, bz).wait_recv()
        return 0

    lax.fori_loop(0, n_z, wait_gl, 0)
    inner = jnp.zeros((1, n_tok), F32)
    for b in range(n_mp):
        at = slice(b * lat_cols, (b + 1) * lat_cols)
        total = own_gl[at, :]
        for i in range(n_mp - 1):
            total = total + peer_gl[i, at, :].astype(F32)
        total = total * gain_b[at, :]
        own_gl[at, :] = total
        inner = inner + jnp.sum(total * lr_t[at, :], axis=0, keepdims=True)
    scale = inner / (lat * root[...] * root[...] * root[...])
    for b in range(n_mp):
        at = slice(b * lat_cols, (b + 1) * lat_cols)
        grad_raw[b] = (own_gl[at, :] / root[...] - lr_t[at, :] * scale).T.astype(BF16)
    for i in range(n_mp - 1):
        w2_share(i, 1 - core).wait_recv()

    def out_part(k, _):
        at = pl.ds(pl.multiple_of(k * r_size, r_size), r_size)
        total = jnp.zeros((n_tok, r_size), F32)
        for b in range(n_mp):
            total = total + lax.dot_general(
                grad_raw[b], wd2[b, at, :], (((1,), (1,)), ((), ())), preferred_element_type=F32
            )
        gt_out[:, at] = total.astype(BF16)
        return 0

    lax.fori_loop(0, 7, out_part, 0)
    gt_store = pltpu.make_async_copy(gt_out, gt_h, out_sem.at[1])
    gt_store.start()

    for kind in (0, 1):

        def drain_own(kind):
            for part in (part_a, part_b):
                for way in (0, 1):
                    z_copy(kind, way, z, part).wait_send()
            c_copy(kind, z, core).wait_send()

        def drain(s, _, kind=kind):
            lz, rz = left(s), right(s)
            z_copy(kind, 0, lz, part_a).wait_send()
            z_copy(kind, 1, rz, part_b).wait_send()

            @pl.when(s < half - 1)
            def _():
                z_copy(kind, 1, rz, part_a).wait_send()
                z_copy(kind, 0, lz, part_b).wait_send()

            for bz in (lz, rz):
                y_copy(kind, bz, part_a).wait_send()
                c_copy(kind, bz, core).wait_send()
            return 0

        drain_own(kind)
        lax.fori_loop(1, half, drain, 0)
        y_copy(kind, far, part_a).wait_send()
        c_copy(kind, far, core).wait_send()

    for i in range(n_mp - 1):
        gain_copy(i).wait_send()
        lr_copy(i, me_x).wait_send()
        w2_copy(i).wait_send()
        w2_share(i, core).wait_send()

    def drain_gl(bz, _):
        for i in range(n_mp - 1):
            gl_copy(i, bz).wait_send()
        return 0

    lax.fori_loop(0, n_z, drain_gl, 0)
    q_store.wait()
    gt_store.wait()


def body(tokens, w_down, gain, w_up, head_counts, cotangent):
    n_dp, n_mp = lax.axis_size("dp"), lax.axis_size("mp")
    n_z = n_dp // 2
    n_tok, width = tokens.shape
    up_rows, cols = w_up.shape
    lat_cols = w_down.shape[1]
    lat = lat_cols * n_mp
    out_cols = width // n_mp
    dma = pltpu.SemaphoreType.DMA
    anywhere = pl.BlockSpec(memory_space=pl.ANY)
    peers = n_mp - 1
    return pl.pallas_call(
        kernel,
        out_shape=(
            jax.ShapeDtypeStruct((n_tok, cols), BF16),
            jax.ShapeDtypeStruct((n_tok, out_cols), BF16),
        ),
        in_specs=[
            anywhere,
            anywhere,
            pl.BlockSpec(memory_space=pltpu.VMEM),
            anywhere,
            pl.BlockSpec(memory_space=pltpu.SMEM),
            anywhere,
        ],
        out_specs=(anywhere, anywhere),
        scratch_shapes=[
            pltpu.VMEM((n_tok, width), BF16),
            pltpu.VMEM((width, lat_cols), BF16),
            pltpu.VMEM((n_mp, out_cols, lat_cols), BF16),
            pltpu.VMEM((lat, cols), BF16),
            pltpu.VMEM((n_tok, cols), BF16),
            pltpu.VMEM((cols, n_tok), BF16),
            pltpu.VMEM((lat, n_tok), F32),
            pltpu.VMEM((lat, n_tok), BF16),
            pltpu.VMEM((lat, n_tok), F32),
            pltpu.VMEM((n_mp, 1, lat_cols), F32),
            pltpu.VMEM((lat, n_tok), F32),
            pltpu.VMEM((lat, n_tok), BF16),
            pltpu.VMEM((peers, lat, n_tok), BF16),
            pltpu.VMEM((n_mp, n_tok, lat_cols), BF16),
            pltpu.VMEM((n_tok, cols), F32),
            pltpu.VMEM((n_tok, cols), BF16),
            pltpu.VMEM((n_tok, out_cols), BF16),
            pltpu.VMEM((1, n_tok), F32),
            dma((4,)),
            dma((2,)),
            dma((2, 2, 3, n_z)),
            dma((2, 3, n_z)),
            dma((2, n_z)),
            dma((2, n_z)),
            dma((2, n_z)),
            dma((peers,)),
            dma((peers,)),
            dma((peers,)),
            dma((peers,)),
            dma((peers,)),
            dma((peers,)),
            dma((peers,)),
            dma((peers,)),
            dma((peers, n_z)),
            dma((peers, n_z)),
        ],
        compiler_params=pltpu.CompilerParams(
            collective_id=0, has_side_effects=True, vmem_limit_bytes=60 * 1024 * 1024
        ),
        name="gather_and_project",
    )(tokens, w_down, gain[None, :], w_up, head_counts, cotangent)


def solution(mesh):
    in_specs = (
        P(("groups", "dp"), None),
        P("dp", "mp"),
        P("mp"),
        P("dp", "mp"),
        P(),
        P(("groups", "dp"), "mp"),
    )
    out_specs = (P(("groups", "dp"), "mp"), P(("groups", "dp"), "mp"))
    return jax.shard_map(body, mesh=mesh, in_specs=in_specs, out_specs=out_specs, check_vma=False)
```

time: 279 us -> 164 us (0.59)
  waiting for transfers between devices: 198 us -> 0 us
  Pallas kernels: 0 us -> 159 us
  matrix products: 29.2 us -> 0 us
  blocking collectives: 19.8 us -> 0 us
  between operations: 14.2 us -> 0.65 us
  starting transfers between devices: 8.15 us -> 0 us
  other arithmetic: 4.13 us -> 0 us
    all_gather x2 -> x0, waiting for transfers between devices: 187 us -> none  [the longest x1 136 us: body(): up_whole = lax.all_gather(w_up, 'dp', axis=0, tiled=True)]
    pallas_call x0 -> x1, Pallas kernels: none -> 159 us  [body(): pl.pallas_call(kernel, out_shape=(jax.ShapeDtypeStruct((n_tok, cols), BF1...]
    dot_general x4 -> x0, matrix products: 29.2 us -> none  [the longest x2 14.6 us: contract_last(): lax.dot_general(left, right, (((1,), (1,)), ((), ())), preferred_element_...]
    all_to_all x1 -> x0, blocking collectives: 11.4 us -> none  [sent_and_summed(): blocks = lax.all_to_all(cut_along(array, dim, size), axis, 0, 0, tiled=True)]
    all_to_all x2 -> x0, waiting for transfers between devices: 8.96 us -> none  [the longest x1 8.65 us: sent_and_summed(): blocks = lax.all_to_all(cut_along(array, dim, size), axis, 0, 0, tiled=True)]
    psum x1 -> x0, blocking collectives: 8.44 us -> none  [body(): lax.psum(jnp.sum(latent_raw * latent_raw, axis=1, keepdims=True), 'mp')]
    all_to_all x2 -> x0, starting transfers between devices: 8.03 us -> none  [the longest x1 4.47 us: sent_and_summed(): blocks = lax.all_to_all(cut_along(array, dim, size), axis, 0, 0, tiled=True)]
    unnamed x4, local copies, waits for them, and re-layouts: 0.02 us -> 3.55 us
  transfers between devices with their start and end apart: 4 -> 0, of which waited for: 4 -> 0; matrix products, arithmetic and copies ran while one was open for 11% -> 0% of each run, Pallas kernels for 0% -> 0%
where the time goes in v1:
time: 164 us
  Pallas kernels  159 us (97%)
  local copies, waits for them, and re-layouts  4.8 us (3%)
    pallas_call x1, Pallas kernels, body(): pl.pallas_call(kernel, out_shape=(jax.ShapeDtypeStruct((n_tok, cols), BF1...  159 us
    unnamed x4, local copies, waits for them, and re-layouts  3.55 us

profile of v1, /device:TPU:33, one launch (start us, length us, event | category | flops | bytes accessed | tf_op | source)
XLA Modules:
  0.0 164.2 jit_solution(13633026037209497502)
XLA Ops:
  0.6 1.2 broadcast_in_dim.3.gain_ref
  1.9 158.8 %gather_and_project.1 = (bf16[128,6528]{1,0:T(8,128)(2,1)}, bf16[128,1792]{1,0:T(8,128)(2,1)}) custom-call(bf16[128,7168]{1,0:T(8,128)(2,1)} %tok_h.1, bf16[224,384]{1,0:T(8,128)(2,1)} %wd_h.1, f32[1,384]{1,0:T(1,128)} %broadcast_in_dim.3.gain_ref, bf16[48,6528]{1,0:T(8,128)(2,1)} %wu_h.1, s32[4]{0:T(128)} %heads_ref.1, bf16[128,6528]{1,0:T(8,128)(2,1)} %cot_h.1), custom_call_target="tpu_custom_call" | custom-call | tf_op jit(solution)/shard_map/gather_and_project/pallas_call | solution.py:439
  160.6 0.0 copy-start
  160.7 2.8 %copy.10 = bf16[128,6528]{1,0:T(8,128)(2,1)} copy(bf16[128,6528]{1,0:T(8,128)(2,1)} %get-tuple-element.4) | data formatting | bytes 3342336
  163.4 0.0 copy-done
  163.4 0.8 copy.11
Async XLA Ops:
  160.6 2.8 %copy-start = (bf16[128,1792]{1,0:T(8,128)(2,1)S(1)}, bf16[128,1792]{1,0:T(8,128)(2,1)}, u32[]{:S(2)}) copy-start(bf16[128,1792]{1,0:T(8,128)(2,1)} %get-tuple-element.5) | copy-start | bytes 1376260

commit v2 on v1

--- a/solution.py
+++ b/solution.py
@@ -11,7 +11,6 @@
 MESH = pl.DeviceIdType.MESH
 F32 = jnp.float32
 BF16 = jnp.bfloat16
-CHUNK = 384
 
 
 def kernel(
@@ -20,6 +19,7 @@
     own_gl, send_gl, peer_gl, grad_raw, q_acc, q_out, gt_out, root,
     load_sem, out_sem, z_send, z_recv, y_send, c_send, c_recv,
     lr_send, lr_recv, ga_send, ga_recv, w2_send, w2_recv, w2c_send, w2c_recv, gl_send, gl_recv,
+    far_send, far_c_send, far_c_recv,
 ):
     n_dp, n_mp = lax.axis_size("dp"), lax.axis_size("mp")
     n_z = n_dp // 2
@@ -91,13 +91,24 @@
         pl.semaphore_signal(barrier, inc=1, device_id=where, device_id_type=MESH)
     pl.semaphore_wait(barrier, len(others))
 
-    def send_own(kind):
+    def send_own_down():
         for part in (part_a, part_b):
             for way in (0, 1):
-                z_copy(kind, way, z, part).start()
-        c_copy(kind, z, core).start()
-
-    def ring_step(kind, s):
+                z_copy(0, way, z, part).start()
+        c_copy(0, z, core).start()
+
+    wide = cols // 3
+
+    def send_own_up(j):
+        part = jnp.where(j < 3, part_a, part_b)
+        rows = pl.ds(pl.multiple_of((2 * z + core) * up_rows + part * rows3, rows3), rows3)
+        ref = wu.at[rows, pl.ds(pl.multiple_of((j % 3) * wide, 128), wide)]
+        for way in (0, 1):
+            remote(
+                ref, ref, z_send.at[1, way, part, z], z_recv.at[1, part, z], {"dp": (after, before)[way]}
+            ).start()
+
+    def ring_step(kind, s, between=None):
         lz, rz = left(s), right(s)
         z_copy(kind, 0, lz, part_a).wait_recv()
         z_copy(kind, 0, lz, part_a).start()
@@ -109,6 +120,8 @@
             z_copy(kind, 1, rz, part_a).start()
 
         y_copy(kind, rz, part_a).start()
+        if between is not None:
+            between()
         z_copy(kind, 0, lz, part_b).wait_recv()
 
         @pl.when(s < half - 1)
@@ -118,11 +131,7 @@
         z_copy(kind, 1, rz, part_b).wait_recv()
         z_copy(kind, 1, rz, part_b).start()
 
-    def last_step(kind):
-        far = right(half)
-        z_copy(kind, 0, far, part_a).wait_recv()
-        y_copy(kind, far, part_a).start()
-        z_copy(kind, 1, far, part_b).wait_recv()
+    far = right(half)
 
     def share(kind, bz):
         y_copy(kind, bz, part_c).wait_recv()
@@ -134,17 +143,37 @@
 
     def wait_sibling(kind, bz):
         c_copy(kind, bz, 1 - core).wait_recv()
+
+    n_lane_tiles = cols // 128
+    cut = (n_lane_tiles + 1) // 2 * 128
+
+    def far_part(bz):
+        return pl.ds(pl.multiple_of((2 * bz + core) * up_rows + part_c * rows3, rows3), rows3)
+
+    def far_copy(way):
+        bz = (left, right)[way](half - 1)
+        ref = wu.at[far_part(bz), (slice(0, cut), slice(cut, cols))[way]]
+        return remote(ref, ref, far_send.at[way], z_recv.at[1, part_c, bz], {"dp": (after, before)[way]})
+
+    def far_share(piece_of, bc):
+        base = (2 * far + bc) * up_rows
+        if piece_of == 0:
+            rows = pl.ds(pl.multiple_of(base + plane * rows3, rows3), 2 * rows3)
+        else:
+            rows = pl.ds(pl.multiple_of(base + part_c * rows3, rows3), rows3)
+        ref = wu.at[rows, :]
+        return remote(ref, ref, far_c_send.at[piece_of], far_c_recv.at[piece_of], {"dp": sibling})
 
     held = jnp.int32(0)
     for i in range(n_mp):
         held = held + jnp.where(me_x == i, heads_ref[i], 0)
     kept = held * HD
-    lane = lax.broadcasted_iota(jnp.int32, (1, CHUNK), 1)
     lane1 = lax.broadcasted_iota(jnp.int32, (1, 128), 1)
 
     own_down.wait()
-    send_own(0)
+    send_own_down()
     own_up.wait()
+    c_copy(1, z, core).start()
     x_peers = [((me_x + i) % n_mp, (me_x + n_mp - i) % n_mp) for i in range(1, n_mp)]
 
     def gain_copy(i):
@@ -152,7 +181,7 @@
             gain_all.at[me_x], gain_all.at[me_x], ga_send.at[i], ga_recv.at[i], {"mp": x_peers[i][0]}
         )
 
-    gain_all[me_x] = gain_ref[...]
+    gain_all[me_x] = gain_ref[...].reshape(1, lat_cols)
     load_cot.wait()
     n_blocks = cols // 128
     per_step = -(-n_blocks // (half - 1))
@@ -164,22 +193,29 @@
         return 0
 
     def down_step(s, _):
-        ring_step(0, s)
+        def between():
+            @pl.when(s > 1)
+            def _():
+                share_pair(0, s - 1)
+
+        ring_step(0, s, between)
+
+        @pl.when(s <= 6)
+        def _():
+            send_own_up(s - 1)
+
         lax.fori_loop((s - 1) * per_step, jnp.minimum(s * per_step, n_blocks), turn, 0)
         return 0
 
     lax.fori_loop(1, half, down_step, 0)
-    send_own(1)
     for i in range(n_mp - 1):
         gain_copy(i).start()
-    last_step(0)
-
-    def share_down(s, _):
-        share_pair(0, s)
-        return 0
-
-    lax.fori_loop(1, half, share_down, 0)
-    share(0, right(half))
+    z_copy(0, 0, far, part_a).wait_recv()
+    y_copy(0, far, part_a).start()
+    z_copy(0, 1, far, part_b).wait_recv()
+    share_pair(0, half - 1)
+    ring_step(1, 1)
+    share(0, far)
     load_tok.wait()
 
     def wait_down(bz, _):
@@ -235,7 +271,8 @@
 
     lax.fori_loop(0, 7, own_part, 0)
 
-    ring_step(1, 1)
+    ring_step(1, 2, lambda: share_pair(1, 1))
+    ring_step(1, 3, lambda: share_pair(1, 2))
 
     for i in range(n_mp - 1):
         ref = gain_all.at[x_peers[i][1]]
@@ -273,80 +310,117 @@
             for i in range(n_mp - 1):
                 gl_copy(i, bz).start()
 
-    def chunk_at(c):
-        return pl.ds(pl.multiple_of(c * CHUNK, CHUNK), CHUNK)
-
-    n_chunks = cols // CHUNK
+    tiles = [(off, min(256, wide - off)) for off in range(0, wide, 256)]
 
     def compute(zs, gl=True, q=True, first=False, final=False):
-        lefts = [lat_t[rows_of(bz), :].T for bz in zs] if q else None
-
-        def step(c, totals):
-            at = chunk_at(c)
-            tiles = [wu[rows_of(bz), at] for bz in zs]
-            if q:
-                value = jnp.dot(lefts[0], tiles[0], preferred_element_type=F32)
-                for one, tile in zip(lefts[1:], tiles[1:]):
-                    value = value + jnp.dot(one, tile, preferred_element_type=F32)
-                if not first:
-                    value = value + q_acc[:, at]
-                if final:
-                    q_out[:, at] = jnp.where(lane + c * CHUNK < kept, value, 0.0).astype(BF16)
-                else:
-                    q_acc[:, at] = value
-            if gl:
-                side = cot_t[at, :]
-                totals = tuple(
-                    total + jnp.dot(tile, side, preferred_element_type=F32) for total, tile in zip(totals, tiles)
-                )
-            return totals
-
-        start = tuple(jnp.zeros((z_rows, n_tok), F32) for _ in zs) if gl else ()
-        totals = lax.fori_loop(0, n_chunks, step, start)
+        if q:
+            one = jnp.concatenate([lat_t[rows_of(bz), :] for bz in zs], axis=0).T
+
+        def step(c, total):
+            for off, size in tiles:
+                at = pl.ds(pl.multiple_of(c * wide + off, 128), size)
+                tile = jnp.concatenate([wu[rows_of(bz), at] for bz in zs], axis=0)
+                if gl:
+                    total = total + jnp.dot(tile, cot_t[at, :], preferred_element_type=F32)
+                if q:
+                    value = jnp.dot(one, tile, preferred_element_type=F32)
+                    if not first:
+                        value = value + q_acc[:, at]
+                    if final:
+                        lane = lax.broadcasted_iota(jnp.int32, (1, size), 1) + (c * wide + off)
+                        q_out[:, at] = jnp.where(lane < kept, value, 0.0).astype(BF16)
+                    else:
+                        q_acc[:, at] = value
+            return total
+
+        start = jnp.zeros((z_rows * len(zs), n_tok), F32) if gl else 0
+        total = lax.fori_loop(0, 3, step, start)
         if gl:
-            for bz, total in zip(zs, totals):
-                publish(bz, total)
+            for k, bz in enumerate(zs):
+                publish(bz, total[k * z_rows : (k + 1) * z_rows])
             send_blocks(zs)
 
-    ring_step(1, 2)
-    share_pair(1, 1)
-    wait_sibling(1, z)
-    compute([z], first=True)
-
-    def up_step(s, _):
-        ring_step(1, s)
-        share_pair(1, s - 1)
-        zs = [left(s - 2), right(s - 2)]
+    def compute_pair(s):
+        zs = [left(s), right(s)]
         for bz in zs:
             wait_sibling(1, bz)
         compute(zs)
-        return 0
-
-    lax.fori_loop(3, half, up_step, 0)
-    last_step(1)
-    share_pair(1, half - 1)
-    zs = [left(half - 2), right(half - 2)]
-    for bz in zs:
-        wait_sibling(1, bz)
-    compute(zs)
-    far = right(half)
-    share(1, far)
-    zs = [left(half - 1), right(half - 1)]
-    for bz in zs:
-        wait_sibling(1, bz)
-    compute(zs)
+
+    wait_sibling(1, z)
+    compute([z], first=True)
+    compute_pair(1)
+    ring_step(1, 4, lambda: share_pair(1, 3))
+
+    def catch_up(s, _):
+        compute_pair(s)
+        return 0
+
+    lax.fori_loop(2, 4, catch_up, 0)
+
+    def up_step(s, _):
+        ring_step(1, s, lambda: share_pair(1, s - 1))
+        compute_pair(s - 1)
+        return 0
+
+    lax.fori_loop(5, half, up_step, 0)
     for i in range(n_mp - 1):
         ref = w2_arrived(i, core)
         remote(ref, ref, w2_send.at[i], w2_recv.at[i], {"mp": x_peers[i][0]}).wait_recv()
         w2_share(i, core).start()
-    wait_sibling(1, far)
+    for way in (0, 1):
+        bz = (left, right)[way](half - 1)
+        y_copy(1, bz, part_c).wait_recv()
+        far_copy(way).start()
+        c_copy(1, bz, core).start()
+    z_copy(1, 0, far, part_a).wait_recv()
+    z_copy(1, 1, far, part_b).wait_recv()
+    far_share(0, core).start()
+    compute_pair(half - 1)
+    z_copy(1, 0, far, part_c).wait_recv()
+    far_share(1, core).start()
+    far_share(0, 1 - core).wait_recv()
+    far_share(1, 1 - core).wait_recv()
     compute([far], q=False)
     compute([far], gl=False, final=True)
     q_store = pltpu.make_async_copy(q_out, q_h, out_sem.at[0])
     q_store.start()
 
+    for kind in (0, 1):
+        for part in (part_a, part_b):
+            for way in (0, 1):
+                z_copy(kind, way, z, part).wait_send()
+        c_copy(kind, z, core).wait_send()
+
+        def drain(s, _, kind=kind):
+            lz, rz = left(s), right(s)
+            z_copy(kind, 0, lz, part_a).wait_send()
+            z_copy(kind, 1, rz, part_b).wait_send()
+
+            @pl.when(s < half - 1)
+            def _():
+                z_copy(kind, 1, rz, part_a).wait_send()
+                z_copy(kind, 0, lz, part_b).wait_send()
+
+            for bz in (lz, rz):
+                y_copy(kind, bz, part_a).wait_send()
+                c_copy(kind, bz, core).wait_send()
+            return 0
+
+        lax.fori_loop(1, half, drain, 0)
+    y_copy(0, far, part_a).wait_send()
+    c_copy(0, far, core).wait_send()
+    for i in range(2):
+        far_copy(i).wait_send()
+        far_share(i, core).wait_send()
+    for i in range(n_mp - 1):
+        gain_copy(i).wait_send()
+        lr_copy(i, me_x).wait_send()
+        w2_copy(i).wait_send()
+        w2_share(i, core).wait_send()
+
     def wait_gl(bz, _):
         for i in range(n_mp - 1):
+            gl_copy(i, bz).wait_send()
             gl_copy(i, bz).wait_recv()
         return 0
 
@@ -367,62 +441,42 @@
     for i in range(n_mp - 1):
         w2_share(i, 1 - core).wait_recv()
 
-    def out_part(k, _):
-        at = pl.ds(pl.multiple_of(k * r_size, r_size), r_size)
+    for k in range(7):
+        at = slice(k * r_size, (k + 1) * r_size)
         total = jnp.zeros((n_tok, r_size), F32)
         for b in range(n_mp):
             total = total + lax.dot_general(
                 grad_raw[b], wd2[b, at, :], (((1,), (1,)), ((), ())), preferred_element_type=F32
             )
         gt_out[:, at] = total.astype(BF16)
-        return 0
-
-    lax.fori_loop(0, 7, out_part, 0)
     gt_store = pltpu.make_async_copy(gt_out, gt_h, out_sem.at[1])
     gt_store.start()
 
-    for kind in (0, 1):
-
-        def drain_own(kind):
-            for part in (part_a, part_b):
-                for way in (0, 1):
-                    z_copy(kind, way, z, part).wait_send()
-            c_copy(kind, z, core).wait_send()
-
-        def drain(s, _, kind=kind):
-            lz, rz = left(s), right(s)
-            z_copy(kind, 0, lz, part_a).wait_send()
-            z_copy(kind, 1, rz, part_b).wait_send()
-
-            @pl.when(s < half - 1)
-            def _():
-                z_copy(kind, 1, rz, part_a).wait_send()
-                z_copy(kind, 0, lz, part_b).wait_send()
-
-            for bz in (lz, rz):
-                y_copy(kind, bz, part_a).wait_send()
-                c_copy(kind, bz, core).wait_send()
-            return 0
-
-        drain_own(kind)
-        lax.fori_loop(1, half, drain, 0)
-        y_copy(kind, far, part_a).wait_send()
-        c_copy(kind, far, core).wait_send()
-
-    for i in range(n_mp - 1):
-        gain_copy(i).wait_send()
-        lr_copy(i, me_x).wait_send()
-        w2_copy(i).wait_send()
-        w2_share(i, core).wait_send()
-
-    def drain_gl(bz, _):
-        for i in range(n_mp - 1):
-            gl_copy(i, bz).wait_send()
-        return 0
-
-    lax.fori_loop(0, n_z, drain_gl, 0)
     q_store.wait()
     gt_store.wait()
+
+
+def write_kernel(q_in, gt_in, q_h, gt_h, q_hold, gt_hold, in_sem, out_sem):
+    n_tok = q_in.shape[0]
+    quarter = n_tok // 4
+    pairs = [(q_in, q_hold, q_h, slice(k * quarter, (k + 1) * quarter)) for k in range(4)]
+    pairs.append((gt_in, gt_hold, gt_h, slice(0, n_tok)))
+
+    def load(k):
+        src, hold, _, at = pairs[k]
+        return pltpu.make_async_copy(src.at[at, :], hold.at[at, :], in_sem.at[k])
+
+    def store(k):
+        _, hold, dst, at = pairs[k]
+        return pltpu.make_async_copy(hold.at[at, :], dst.at[at, :], out_sem.at[k])
+
+    for k in range(len(pairs)):
+        load(k).start()
+    for k in range(len(pairs)):
+        load(k).wait()
+        store(k).start()
+    for k in range(len(pairs)):
+        store(k).wait()
 
 
 def body(tokens, w_down, gain, w_up, head_counts, cotangent):
@@ -436,7 +490,7 @@
     dma = pltpu.SemaphoreType.DMA
     anywhere = pl.BlockSpec(memory_space=pl.ANY)
     peers = n_mp - 1
-    return pl.pallas_call(
+    queries, grad_tokens = pl.pallas_call(
         kernel,
         out_shape=(
             jax.ShapeDtypeStruct((n_tok, cols), BF16),
@@ -487,12 +541,31 @@
             dma((peers,)),
             dma((peers, n_z)),
             dma((peers, n_z)),
+            dma((2,)),
+            dma((2,)),
+            dma((2,)),
         ],
         compiler_params=pltpu.CompilerParams(
             collective_id=0, has_side_effects=True, vmem_limit_bytes=60 * 1024 * 1024
         ),
         name="gather_and_project",
-    )(tokens, w_down, gain[None, :], w_up, head_counts, cotangent)
+    )(tokens, w_down, gain, w_up, head_counts, cotangent)
+    return pl.pallas_call(
+        write_kernel,
+        out_shape=(
+            jax.ShapeDtypeStruct((n_tok, cols), BF16),
+            jax.ShapeDtypeStruct((n_tok, out_cols), BF16),
+        ),
+        in_specs=[anywhere, anywhere],
+        out_specs=(anywhere, anywhere),
+        scratch_shapes=[
+            pltpu.VMEM((n_tok, cols), BF16),
+            pltpu.VMEM((n_tok, out_cols), BF16),
+            dma((5,)),
+            dma((5,)),
+        ],
+        name="write_outputs",
+    )(queries, grad_tokens)
 
 
 def solution(mesh):

time: 164 us -> 143 us (0.87)
  Pallas kernels: 159 us -> 142 us
  local copies, waits for them, and re-layouts: 4.8 us -> 0 us
    pallas_call x1, Pallas kernels: 159 us -> 140 us  [body(): pl.pallas_call(kernel, out_shape=(jax.ShapeDtypeStruct((n_tok, cols), BF1...]
    unnamed x4 -> x0, local copies, waits for them, and re-layouts: 3.55 us -> none
    pallas_call x0 -> x1, Pallas kernels: none -> 2.41 us  [body(): pl.pallas_call(write_kernel, out_shape=(jax.ShapeDtypeStruct((n_tok, cols...]
where the time goes in v2:
time: 143 us
  Pallas kernels  142 us (99%)
    pallas_call x1, Pallas kernels, body(): pl.pallas_call(kernel, out_shape=(jax.ShapeDtypeStruct((n_tok, cols), BF1...  140 us

profile of v2, /device:TPU:33, one launch (start us, length us, event | category | flops | bytes accessed | tf_op | source)
XLA Modules:
  0.0 142.9 jit_solution(3243701253349861751)
XLA Ops:
  0.6 139.9 %gather_and_project.1 = (bf16[128,6528]{1,0:T(8,128)(2,1)}, bf16[128,1792]{1,0:T(8,128)(2,1)}) custom-call(bf16[128,7168]{1,0:T(8,128)(2,1)} %tok_h.1, bf16[224,384]{1,0:T(8,128)(2,1)} %wd_h.1, f32[384]{0:T(512)} %gain_ref.1, bf16[48,6528]{1,0:T(8,128)(2,1)} %wu_h.1, s32[4]{0:T(128)} %heads_ref.1, bf16[128,6528]{1,0:T(8,128)(2,1)} %cot_h.1), custom_call_target="tpu_custom_call" | custom-call | tf_op jit(solution)/shard_map/gather_and_project/pallas_call | solution.py:493
  140.5 2.4 %write_outputs.1 = (bf16[128,6528]{1,0:T(8,128)(2,1)}, bf16[128,1792]{1,0:T(8,128)(2,1)}) custom-call(bf16[128,6528]{1,0:T(8,128)(2,1)} %get-tuple-element.4.q_in, bf16[128,1792]{1,0:T(8,128)(2,1)} %get-tuple-element.5.gt_in), custom_call_target="tpu_custom_call" | custom-call | tf_op jit(solution)/shard_map/write_outputs/pallas_call | solution.py:553

commit v3 on v2

--- a/solution.py
+++ b/solution.py
@@ -14,12 +14,12 @@
 
 
 def kernel(
-    tok_h, wd_h, gain_ref, wu_h, heads_ref, cot_h, q_h, gt_h,
+    tok_h, wd_h, gain_h, wu_h, heads_h, cot_h, q_h, gt_h,
     tok, wd, wd2, wu, cot, cot_t, lr_t, lat_t, gain_b, gain_all,
     own_gl, send_gl, peer_gl, grad_raw, q_acc, q_out, gt_out, root,
     load_sem, out_sem, z_send, z_recv, y_send, c_send, c_recv,
     lr_send, lr_recv, ga_send, ga_recv, w2_send, w2_recv, w2c_send, w2c_recv, gl_send, gl_recv,
-    far_send, far_c_send, far_c_recv,
+    far_send, far_c_send, far_c_recv, gain_ref, heads_ref,
 ):
     n_dp, n_mp = lax.axis_size("dp"), lax.axis_size("mp")
     n_z = n_dp // 2
@@ -81,6 +81,10 @@
     load_tok = pltpu.make_async_copy(tok_h, tok, load_sem.at[3])
     own_down.start()
     own_up.start()
+    load_gain = pltpu.make_async_copy(gain_h, gain_ref, load_sem.at[4])
+    load_heads = pltpu.make_async_copy(heads_h, heads_ref, load_sem.at[5])
+    load_gain.start()
+    load_heads.start()
     load_cot.start()
     load_tok.start()
 
@@ -108,7 +112,7 @@
                 ref, ref, z_send.at[1, way, part, z], z_recv.at[1, part, z], {"dp": (after, before)[way]}
             ).start()
 
-    def ring_step(kind, s, between=None):
+    def ring_a(kind, s):
         lz, rz = left(s), right(s)
         z_copy(kind, 0, lz, part_a).wait_recv()
         z_copy(kind, 0, lz, part_a).start()
@@ -120,8 +124,9 @@
             z_copy(kind, 1, rz, part_a).start()
 
         y_copy(kind, rz, part_a).start()
-        if between is not None:
-            between()
+
+    def ring_b(kind, s):
+        lz, rz = left(s), right(s)
         z_copy(kind, 0, lz, part_b).wait_recv()
 
         @pl.when(s < half - 1)
@@ -131,11 +136,42 @@
         z_copy(kind, 1, rz, part_b).wait_recv()
         z_copy(kind, 1, rz, part_b).start()
 
+    def ring_step(kind, s, between):
+        ring_a(kind, s)
+        between()
+        ring_b(kind, s)
+
     far = right(half)
+
+    x_peers = [((me_x + i) % n_mp, (me_x + n_mp - i) % n_mp) for i in range(1, n_mp)]
+    per_x = n_z // n_mp
+
+    def w2_at(owner, j, bc):
+        return wd2.at[owner, pl.ds(pl.multiple_of((2 * j + bc) * down_rows, down_rows), down_rows), :]
+
+    def w2_copy(bz):
+        to = bz // per_x
+        j = bz - to * per_x
+        slot = (to + n_mp - 1 - me_x) % n_mp
+        return remote(block(0, bz, core), w2_at(me_x, j, core), w2_send.at[bz], w2_recv.at[slot, j], {"mp": to})
+
+    def pass_on(bz):
+        @pl.when(bz // per_x != me_x)
+        def _():
+            w2_copy(bz).start()
+
+    def w2_rows(i, j, bc):
+        return w2_at(x_peers[i][1], j, bc)
+
+    def w2_share(i, j, bc):
+        ref = w2_rows(i, j, bc)
+        return remote(ref, ref, w2c_send.at[i, j], w2c_recv.at[i, j], {"dp": sibling})
 
     def share(kind, bz):
         y_copy(kind, bz, part_c).wait_recv()
         c_copy(kind, bz, core).start()
+        if kind == 0:
+            pass_on(bz)
 
     def share_pair(kind, s):
         share(kind, left(s))
@@ -145,7 +181,7 @@
         c_copy(kind, bz, 1 - core).wait_recv()
 
     n_lane_tiles = cols // 128
-    cut = (n_lane_tiles + 1) // 2 * 128
+    cut = n_lane_tiles * 2 // 3 * 128
 
     def far_part(bz):
         return pl.ds(pl.multiple_of((2 * bz + core) * up_rows + part_c * rows3, rows3), rows3)
@@ -164,23 +200,25 @@
         ref = wu.at[rows, :]
         return remote(ref, ref, far_c_send.at[piece_of], far_c_recv.at[piece_of], {"dp": sibling})
 
+    lane1 = lax.broadcasted_iota(jnp.int32, (1, 128), 1)
+
+    own_down.wait()
+    send_own_down()
+    own_up.wait()
+    send_own_up(0)
+    pass_on(z)
+    c_copy(1, z, core).start()
+    def gain_copy(i):
+        return remote(
+            gain_all.at[me_x], gain_all.at[me_x], ga_send.at[i], ga_recv.at[i], {"mp": x_peers[i][0]}
+        )
+
+    load_gain.wait()
+    load_heads.wait()
     held = jnp.int32(0)
     for i in range(n_mp):
         held = held + jnp.where(me_x == i, heads_ref[i], 0)
     kept = held * HD
-    lane1 = lax.broadcasted_iota(jnp.int32, (1, 128), 1)
-
-    own_down.wait()
-    send_own_down()
-    own_up.wait()
-    c_copy(1, z, core).start()
-    x_peers = [((me_x + i) % n_mp, (me_x + n_mp - i) % n_mp) for i in range(1, n_mp)]
-
-    def gain_copy(i):
-        return remote(
-            gain_all.at[me_x], gain_all.at[me_x], ga_send.at[i], ga_recv.at[i], {"mp": x_peers[i][0]}
-        )
-
     gain_all[me_x] = gain_ref[...].reshape(1, lat_cols)
     load_cot.wait()
     n_blocks = cols // 128
@@ -194,28 +232,49 @@
 
     def down_step(s, _):
         def between():
-            @pl.when(s > 1)
+            @pl.when(s > 2)
             def _():
-                share_pair(0, s - 1)
+                share_pair(0, s - 2)
 
         ring_step(0, s, between)
 
-        @pl.when(s <= 6)
-        def _():
-            send_own_up(s - 1)
+        @pl.when(s <= 5)
+        def _():
+            send_own_up(s)
+
+        @pl.when(s == 4)
+        def _():
+            z_copy(1, 0, left(1), part_a).wait_recv()
+            y_copy(1, left(1), part_a).start()
+
+        @pl.when(s == 5)
+        def _():
+            z_copy(1, 1, right(1), part_a).wait_recv()
+            y_copy(1, right(1), part_a).start()
+
+        @pl.when(s == 6)
+        def _():
+            z_copy(1, 0, left(1), part_a).start()
+            z_copy(1, 1, right(1), part_a).start()
 
         lax.fori_loop((s - 1) * per_step, jnp.minimum(s * per_step, n_blocks), turn, 0)
         return 0
 
     lax.fori_loop(1, half, down_step, 0)
+    z_copy(1, 0, left(1), part_b).wait_recv()
+    z_copy(1, 0, left(1), part_b).start()
+    z_copy(1, 1, right(1), part_b).wait_recv()
+    z_copy(1, 1, right(1), part_b).start()
     for i in range(n_mp - 1):
         gain_copy(i).start()
     z_copy(0, 0, far, part_a).wait_recv()
     y_copy(0, far, part_a).start()
     z_copy(0, 1, far, part_b).wait_recv()
+    ring_a(1, 2)
+    share_pair(0, half - 2)
     share_pair(0, half - 1)
-    ring_step(1, 1)
     share(0, far)
+    ring_b(1, 2)
     load_tok.wait()
 
     def wait_down(bz, _):
@@ -241,55 +300,8 @@
         ref = lr_t.at[lat_rows(owner), :]
         return remote(ref, ref, lr_send.at[i], lr_recv.at[i], {"mp": x_peers[i][0]})
 
-    half_out = out_cols // 2
-
-    def w2_copy(i):
-        to, came_from = x_peers[i]
-        rows = pl.ds(pl.multiple_of(to * out_cols + core * half_out, half_out), half_out)
-        mine = pl.ds(pl.multiple_of(core * half_out, half_out), half_out)
-        return remote(wd.at[rows, :], wd2.at[me_x, mine, :], w2_send.at[i], w2_recv.at[i], {"mp": to})
-
-    def w2_arrived(i, bc):
-        rows = pl.ds(pl.multiple_of(bc * half_out, half_out), half_out)
-        return wd2.at[x_peers[i][1], rows, :]
-
-    def w2_share(i, bc):
-        ref = w2_arrived(i, bc)
-        return remote(ref, ref, w2c_send.at[i], w2c_recv.at[i], {"dp": sibling})
-
     for i in range(n_mp - 1):
         lr_copy(i, me_x).start()
-    for i in range(n_mp - 1):
-        w2_copy(i).start()
-    r_size = out_cols // 7
-
-    def own_part(k, _):
-        to = pl.ds(pl.multiple_of(k * r_size, r_size), r_size)
-        came = pl.ds(pl.multiple_of(me_x * out_cols + k * r_size, r_size), r_size)
-        wd2[me_x, to, :] = wd[came, :]
-        return 0
-
-    lax.fori_loop(0, 7, own_part, 0)
-
-    ring_step(1, 2, lambda: share_pair(1, 1))
-    ring_step(1, 3, lambda: share_pair(1, 2))
-
-    for i in range(n_mp - 1):
-        ref = gain_all.at[x_peers[i][1]]
-        remote(ref, ref, ga_send.at[i], ga_recv.at[i], {"mp": x_peers[i][0]}).wait_recv()
-    for b in range(n_mp):
-        gain_b[b * lat_cols : (b + 1) * lat_cols, :] = jnp.broadcast_to(gain_all[b], (n_tok, lat_cols)).T
-    for i in range(n_mp - 1):
-        lr_copy(i, x_peers[i][1]).wait_recv()
-    squares = jnp.zeros((1, n_tok), F32)
-    for b in range(n_mp):
-        value = lr_t[b * lat_cols : (b + 1) * lat_cols, :]
-        squares = squares + jnp.sum(value * value, axis=0, keepdims=True)
-    root[...] = jnp.sqrt(squares / lat + 1e-06)
-    for b in range(n_mp):
-        at = slice(b * lat_cols, (b + 1) * lat_cols)
-        lat_t[at, :] = (lr_t[at, :] / root[...] * gain_b[at, :]).astype(BF16)
-
     z_rows = 2 * up_rows
 
     def rows_of(bz):
@@ -340,33 +352,78 @@
                 publish(bz, total[k * z_rows : (k + 1) * z_rows])
             send_blocks(zs)
 
-    def compute_pair(s):
-        zs = [left(s), right(s)]
-        for bz in zs:
+    def pair(s):
+        return [left(s), right(s)]
+
+    def gl_pair(s):
+        for bz in pair(s):
             wait_sibling(1, bz)
-        compute(zs)
-
+        compute(pair(s), q=False)
+
+    def q_pair(s):
+        compute(pair(s), gl=False)
+
+    ring_a(1, 3)
+    share_pair(1, 1)
+    share_pair(1, 2)
     wait_sibling(1, z)
-    compute([z], first=True)
-    compute_pair(1)
-    ring_step(1, 4, lambda: share_pair(1, 3))
-
-    def catch_up(s, _):
-        compute_pair(s)
-        return 0
-
-    lax.fori_loop(2, 4, catch_up, 0)
-
-    def up_step(s, _):
+    compute([z], q=False)
+    ring_b(1, 3)
+    gl_pair(1)
+    r_size = out_cols // 7
+
+    def own_part(k, _):
+        to = pl.ds(pl.multiple_of(k * r_size, r_size), r_size)
+        came = pl.ds(pl.multiple_of(me_x * out_cols + k * r_size, r_size), r_size)
+        wd2[me_x, to, :] = wd[came, :]
+        return 0
+
+    lax.fori_loop(0, 7, own_part, 0)
+    ring_a(1, 4)
+    share_pair(1, 3)
+    gl_pair(2)
+    ring_b(1, 4)
+
+    def w2_pass(j, _):
+        for i in range(n_mp - 1):
+            ref = w2_rows(i, j, core)
+            remote(ref, ref, w2_send.at[j], w2_recv.at[i, j], {"mp": x_peers[i][0]}).wait_recv()
+            w2_share(i, j, core).start()
+        return 0
+
+    def middle(s, _):
+        gl_pair(s - 2)
         ring_step(1, s, lambda: share_pair(1, s - 1))
-        compute_pair(s - 1)
-        return 0
-
-    lax.fori_loop(5, half, up_step, 0)
+        return 0
+
+    lax.fori_loop(5, 7, middle, 0)
+    gl_pair(5)
     for i in range(n_mp - 1):
-        ref = w2_arrived(i, core)
-        remote(ref, ref, w2_send.at[i], w2_recv.at[i], {"mp": x_peers[i][0]}).wait_recv()
-        w2_share(i, core).start()
+        ref = gain_all.at[x_peers[i][1]]
+        remote(ref, ref, ga_send.at[i], ga_recv.at[i], {"mp": x_peers[i][0]}).wait_recv()
+    for b in range(n_mp):
+        gain_b[b * lat_cols : (b + 1) * lat_cols, :] = jnp.broadcast_to(gain_all[b], (n_tok, lat_cols)).T
+    for i in range(n_mp - 1):
+        lr_copy(i, x_peers[i][1]).wait_recv()
+    squares = jnp.zeros((1, n_tok), F32)
+    for b in range(n_mp):
+        value = lr_t[b * lat_cols : (b + 1) * lat_cols, :]
+        squares = squares + jnp.sum(value * value, axis=0, keepdims=True)
+    root[...] = jnp.sqrt(squares / lat + 1e-06)
+    for b in range(n_mp):
+        at = slice(b * lat_cols, (b + 1) * lat_cols)
+        lat_t[at, :] = (lr_t[at, :] / root[...] * gain_b[at, :]).astype(BF16)
+
+    compute([z], gl=False, first=True)
+    q_pair(1)
+    ring_a(1, 7)
+    share_pair(1, 6)
+    q_pair(2)
+    q_pair(3)
+    ring_b(1, 7)
+    gl_pair(6)
+    q_pair(4)
+    lax.fori_loop(0, per_x, w2_pass, 0)
     for way in (0, 1):
         bz = (left, right)[way](half - 1)
         y_copy(1, bz, part_c).wait_recv()
@@ -375,12 +432,15 @@
     z_copy(1, 0, far, part_a).wait_recv()
     z_copy(1, 1, far, part_b).wait_recv()
     far_share(0, core).start()
-    compute_pair(half - 1)
+    gl_pair(half - 1)
+    q_pair(5)
     z_copy(1, 0, far, part_c).wait_recv()
     far_share(1, core).start()
+    q_pair(6)
     far_share(0, 1 - core).wait_recv()
     far_share(1, 1 - core).wait_recv()
     compute([far], q=False)
+    q_pair(7)
     compute([far], gl=False, final=True)
     q_store = pltpu.make_async_copy(q_out, q_h, out_sem.at[0])
     q_store.start()
@@ -415,8 +475,17 @@
     for i in range(n_mp - 1):
         gain_copy(i).wait_send()
         lr_copy(i, me_x).wait_send()
-        w2_copy(i).wait_send()
-        w2_share(i, core).wait_send()
+        for j in range(per_x):
+            w2_share(i, j, core).wait_send()
+
+    def drain_w2(bz, _):
+        @pl.when(bz // per_x != me_x)
+        def _():
+            w2_copy(bz).wait_send()
+
+        return 0
+
+    lax.fori_loop(0, n_z, drain_w2, 0)
 
     def wait_gl(bz, _):
         for i in range(n_mp - 1):
@@ -439,7 +508,8 @@
         at = slice(b * lat_cols, (b + 1) * lat_cols)
         grad_raw[b] = (own_gl[at, :] / root[...] - lr_t[at, :] * scale).T.astype(BF16)
     for i in range(n_mp - 1):
-        w2_share(i, 1 - core).wait_recv()
+        for j in range(per_x):
+            w2_share(i, j, 1 - core).wait_recv()
 
     for k in range(7):
         at = slice(k * r_size, (k + 1) * r_size)
@@ -499,9 +569,9 @@
         in_specs=[
             anywhere,
             anywhere,
-            pl.BlockSpec(memory_space=pltpu.VMEM),
             anywhere,
-            pl.BlockSpec(memory_space=pltpu.SMEM),
+            anywhere,
+            anywhere,
             anywhere,
         ],
         out_specs=(anywhere, anywhere),
@@ -524,7 +594,7 @@
             pltpu.VMEM((n_tok, cols), BF16),
             pltpu.VMEM((n_tok, out_cols), BF16),
             pltpu.VMEM((1, n_tok), F32),
-            dma((4,)),
+            dma((6,)),
             dma((2,)),
             dma((2, 2, 3, n_z)),
             dma((2, 3, n_z)),
@@ -535,15 +605,17 @@
             dma((peers,)),
             dma((peers,)),
             dma((peers,)),
-            dma((peers,)),
-            dma((peers,)),
-            dma((peers,)),
-            dma((peers,)),
+            dma((n_z,)),
+            dma((peers, n_z // n_mp)),
+            dma((peers, n_z // n_mp)),
+            dma((peers, n_z // n_mp)),
             dma((peers, n_z)),
             dma((peers, n_z)),
             dma((2,)),
             dma((2,)),
             dma((2,)),
+            pltpu.VMEM(gain.shape, F32),
+            pltpu.SMEM(head_counts.shape, jnp.int32),
         ],
         compiler_params=pltpu.CompilerParams(
             collective_id=0, has_side_effects=True, vmem_limit_bytes=60 * 1024 * 1024

time: 143 us -> 137 us (0.958)
  Pallas kernels: 142 us -> 136 us
    pallas_call x1, Pallas kernels: 140 us -> 134 us  [body(): pl.pallas_call(kernel, out_shape=(jax.ShapeDtypeStruct((n_tok, cols), BF1...]
where the time goes in v3:
time: 137 us
  Pallas kernels  136 us (99%)
    pallas_call x1, Pallas kernels, body(): pl.pallas_call(kernel, out_shape=(jax.ShapeDtypeStruct((n_tok, cols), BF1...  134 us

profile of v3, /device:TPU:33, one launch (start us, length us, event | category | flops | bytes accessed | tf_op | source)
XLA Modules:
  0.0 136.7 jit_solution(763715343720624917)
XLA Ops:
  0.6 133.7 %gather_and_project.1 = (bf16[128,6528]{1,0:T(8,128)(2,1)}, bf16[128,1792]{1,0:T(8,128)(2,1)}) custom-call(bf16[128,7168]{1,0:T(8,128)(2,1)} %tok_h.1, bf16[224,384]{1,0:T(8,128)(2,1)} %wd_h.1, f32[384]{0:T(512)} %gain_h.1, bf16[48,6528]{1,0:T(8,128)(2,1)} %wu_h.1, s32[4]{0:T(128)} %heads_h.1, bf16[128,6528]{1,0:T(8,128)(2,1)} %cot_h.1), custom_call_target="tpu_custom_call" | custom-call | tf_op jit(solution)/shard_map/gather_and_project/pallas_call | solution.py:563
  134.3 2.4 %write_outputs.1 = (bf16[128,6528]{1,0:T(8,128)(2,1)}, bf16[128,1792]{1,0:T(8,128)(2,1)}) custom-call(bf16[128,6528]{1,0:T(8,128)(2,1)} %get-tuple-element.4.q_in, bf16[128,1792]{1,0:T(8,128)(2,1)} %get-tuple-element.5.gt_in), custom_call_target="tpu_custom_call" | custom-call | tf_op jit(solution)/shard_map/write_outputs/pallas_call | solution.py:625

commit v4 on v3

--- a/solution.py
+++ b/solution.py
@@ -19,7 +19,7 @@
     own_gl, send_gl, peer_gl, grad_raw, q_acc, q_out, gt_out, root,
     load_sem, out_sem, z_send, z_recv, y_send, c_send, c_recv,
     lr_send, lr_recv, ga_send, ga_recv, w2_send, w2_recv, w2c_send, w2c_recv, gl_send, gl_recv,
-    far_send, far_c_send, far_c_recv, gain_ref, heads_ref,
+    far_send, gain_ref, heads_ref,
 ):
     n_dp, n_mp = lax.axis_size("dp"), lax.axis_size("mp")
     n_z = n_dp // 2
@@ -58,16 +58,25 @@
     def z_copy(kind, way, bz, part):
         ref = piece(kind, bz, part)
         return remote(
-            ref, ref, z_send.at[kind, way, part, bz], z_recv.at[kind, part, bz], {"dp": (after, before)[way]}
+            ref, ref, z_send.at[kind], z_recv.at[kind, part, bz], {"dp": (after, before)[way]}
         )
 
     def y_copy(kind, bz, part):
         ref = piece(kind, bz, part)
-        return remote(ref, ref, y_send.at[kind, bz], z_recv.at[kind, part, bz], {"groups": partner})
+        return remote(ref, ref, y_send.at[kind], z_recv.at[kind, part, bz], {"groups": partner})
 
     def c_copy(kind, bz, bc):
         ref = block(kind, bz, bc)
-        return remote(ref, ref, c_send.at[kind, bz], c_recv.at[kind, bz], {"dp": sibling})
+        return remote(ref, ref, c_send.at[kind], c_recv.at[bz if kind else n_z], {"dp": sibling})
+
+    def c_part(bz, which):
+        base = (2 * bz + core) * up_rows
+        if which == 0:
+            rows = pl.ds(pl.multiple_of(base + plane * rows3, rows3), 2 * rows3)
+        else:
+            rows = pl.ds(pl.multiple_of(base + part_c * rows3, rows3), rows3)
+        ref = wu.at[rows, :]
+        return remote(ref, ref, c_send.at[1], c_recv.at[bz], {"dp": sibling})
 
     def left(s):
         return (z + n_z - s) % n_z
@@ -109,7 +118,7 @@
         ref = wu.at[rows, pl.ds(pl.multiple_of((j % 3) * wide, 128), wide)]
         for way in (0, 1):
             remote(
-                ref, ref, z_send.at[1, way, part, z], z_recv.at[1, part, z], {"dp": (after, before)[way]}
+                ref, ref, z_send.at[1], z_recv.at[1, part, z], {"dp": (after, before)[way]}
             ).start()
 
     def ring_a(kind, s):
@@ -135,6 +144,9 @@
 
         z_copy(kind, 1, rz, part_b).wait_recv()
         z_copy(kind, 1, rz, part_b).start()
+        if kind == 1:
+            c_part(lz, 0).start()
+            c_part(rz, 0).start()
 
     def ring_step(kind, s, between):
         ring_a(kind, s)
@@ -152,8 +164,7 @@
     def w2_copy(bz):
         to = bz // per_x
         j = bz - to * per_x
-        slot = (to + n_mp - 1 - me_x) % n_mp
-        return remote(block(0, bz, core), w2_at(me_x, j, core), w2_send.at[bz], w2_recv.at[slot, j], {"mp": to})
+        return remote(block(0, bz, core), w2_at(me_x, j, core), w2_send.at[0], w2_recv.at[0], {"mp": to})
 
     def pass_on(bz):
         @pl.when(bz // per_x != me_x)
@@ -165,13 +176,15 @@
 
     def w2_share(i, j, bc):
         ref = w2_rows(i, j, bc)
-        return remote(ref, ref, w2c_send.at[i, j], w2c_recv.at[i, j], {"dp": sibling})
+        return remote(ref, ref, w2c_send.at[0], w2c_recv.at[0], {"dp": sibling})
 
     def share(kind, bz):
         y_copy(kind, bz, part_c).wait_recv()
-        c_copy(kind, bz, core).start()
         if kind == 0:
+            c_copy(0, bz, core).start()
             pass_on(bz)
+        else:
+            c_part(bz, 1).start()
 
     def share_pair(kind, s):
         share(kind, left(s))
@@ -189,16 +202,7 @@
     def far_copy(way):
         bz = (left, right)[way](half - 1)
         ref = wu.at[far_part(bz), (slice(0, cut), slice(cut, cols))[way]]
-        return remote(ref, ref, far_send.at[way], z_recv.at[1, part_c, bz], {"dp": (after, before)[way]})
-
-    def far_share(piece_of, bc):
-        base = (2 * far + bc) * up_rows
-        if piece_of == 0:
-            rows = pl.ds(pl.multiple_of(base + plane * rows3, rows3), 2 * rows3)
-        else:
-            rows = pl.ds(pl.multiple_of(base + part_c * rows3, rows3), rows3)
-        ref = wu.at[rows, :]
-        return remote(ref, ref, far_c_send.at[piece_of], far_c_recv.at[piece_of], {"dp": sibling})
+        return remote(ref, ref, far_send.at[0], z_recv.at[1, part_c, bz], {"dp": (after, before)[way]})
 
     lane1 = lax.broadcasted_iota(jnp.int32, (1, 128), 1)
 
@@ -210,7 +214,7 @@
     c_copy(1, z, core).start()
     def gain_copy(i):
         return remote(
-            gain_all.at[me_x], gain_all.at[me_x], ga_send.at[i], ga_recv.at[i], {"mp": x_peers[i][0]}
+            gain_all.at[me_x], gain_all.at[me_x], ga_send.at[0], ga_recv.at[0], {"mp": x_peers[i][0]}
         )
 
     load_gain.wait()
@@ -265,6 +269,8 @@
     z_copy(1, 0, left(1), part_b).start()
     z_copy(1, 1, right(1), part_b).wait_recv()
     z_copy(1, 1, right(1), part_b).start()
+    c_part(left(1), 0).start()
+    c_part(right(1), 0).start()
     for i in range(n_mp - 1):
         gain_copy(i).start()
     z_copy(0, 0, far, part_a).wait_recv()
@@ -277,11 +283,8 @@
     ring_b(1, 2)
     load_tok.wait()
 
-    def wait_down(bz, _):
-        wait_sibling(0, bz)
-        return 0
-
-    lax.fori_loop(0, n_z, wait_down, 0)
+    from_sibling = wd.at[pl.ds(0, n_z * down_rows), :]
+    remote(from_sibling, from_sibling, c_send.at[0], c_recv.at[n_z], {"dp": sibling}).wait_recv()
 
     k_size = width // 7
 
@@ -298,7 +301,7 @@
 
     def lr_copy(i, owner):
         ref = lr_t.at[lat_rows(owner), :]
-        return remote(ref, ref, lr_send.at[i], lr_recv.at[i], {"mp": x_peers[i][0]})
+        return remote(ref, ref, lr_send.at[0], lr_recv.at[0], {"mp": x_peers[i][0]})
 
     for i in range(n_mp - 1):
         lr_copy(i, me_x).start()
@@ -310,7 +313,7 @@
     def gl_copy(i, bz):
         return remote(
             send_gl.at[rows_of(bz), :], peer_gl.at[i, rows_of(bz), :],
-            gl_send.at[i, bz], gl_recv.at[i, bz], {"mp": x_peers[i][0]},
+            gl_send.at[0], gl_recv.at[0], {"mp": x_peers[i][0]},
         )
 
     def publish(bz, value):
@@ -384,10 +387,13 @@
     gl_pair(2)
     ring_b(1, 4)
 
+    def whole(ref, send, recv):
+        return remote(ref, ref, send.at[0], recv.at[0], {"dp": sibling})
+
+    w2_bytes = wd.at[pl.ds(0, (n_mp - 1) * per_x * down_rows), :]
+
     def w2_pass(j, _):
         for i in range(n_mp - 1):
-            ref = w2_rows(i, j, core)
-            remote(ref, ref, w2_send.at[j], w2_recv.at[i, j], {"mp": x_peers[i][0]}).wait_recv()
             w2_share(i, j, core).start()
         return 0
 
@@ -398,13 +404,12 @@
 
     lax.fori_loop(5, 7, middle, 0)
     gl_pair(5)
-    for i in range(n_mp - 1):
-        ref = gain_all.at[x_peers[i][1]]
-        remote(ref, ref, ga_send.at[i], ga_recv.at[i], {"mp": x_peers[i][0]}).wait_recv()
+    gain_bytes = gain_all.at[pl.ds(0, n_mp - 1)]
+    lat_bytes = lr_t.at[pl.ds(0, (n_mp - 1) * lat_cols), :]
+    whole(gain_bytes, ga_send, ga_recv).wait_recv()
     for b in range(n_mp):
         gain_b[b * lat_cols : (b + 1) * lat_cols, :] = jnp.broadcast_to(gain_all[b], (n_tok, lat_cols)).T
-    for i in range(n_mp - 1):
-        lr_copy(i, x_peers[i][1]).wait_recv()
+    whole(lat_bytes, lr_send, lr_recv).wait_recv()
     squares = jnp.zeros((1, n_tok), F32)
     for b in range(n_mp):
         value = lr_t[b * lat_cols : (b + 1) * lat_cols, :]
@@ -423,77 +428,46 @@
     ring_b(1, 7)
     gl_pair(6)
     q_pair(4)
+    whole(w2_bytes, w2_send, w2_recv).wait_recv()
     lax.fori_loop(0, per_x, w2_pass, 0)
     for way in (0, 1):
         bz = (left, right)[way](half - 1)
         y_copy(1, bz, part_c).wait_recv()
         far_copy(way).start()
-        c_copy(1, bz, core).start()
+        c_part(bz, 1).start()
     z_copy(1, 0, far, part_a).wait_recv()
     z_copy(1, 1, far, part_b).wait_recv()
-    far_share(0, core).start()
+    c_part(far, 0).start()
     gl_pair(half - 1)
     q_pair(5)
     z_copy(1, 0, far, part_c).wait_recv()
-    far_share(1, core).start()
+    c_part(far, 1).start()
     q_pair(6)
-    far_share(0, 1 - core).wait_recv()
-    far_share(1, 1 - core).wait_recv()
+    wait_sibling(1, far)
     compute([far], q=False)
     q_pair(7)
     compute([far], gl=False, final=True)
     q_store = pltpu.make_async_copy(q_out, q_h, out_sem.at[0])
     q_store.start()
 
-    for kind in (0, 1):
-        for part in (part_a, part_b):
-            for way in (0, 1):
-                z_copy(kind, way, z, part).wait_send()
-        c_copy(kind, z, core).wait_send()
-
-        def drain(s, _, kind=kind):
-            lz, rz = left(s), right(s)
-            z_copy(kind, 0, lz, part_a).wait_send()
-            z_copy(kind, 1, rz, part_b).wait_send()
-
-            @pl.when(s < half - 1)
-            def _():
-                z_copy(kind, 1, rz, part_a).wait_send()
-                z_copy(kind, 0, lz, part_b).wait_send()
-
-            for bz in (lz, rz):
-                y_copy(kind, bz, part_a).wait_send()
-                c_copy(kind, bz, core).wait_send()
-            return 0
-
-        lax.fori_loop(1, half, drain, 0)
-    y_copy(0, far, part_a).wait_send()
-    c_copy(0, far, core).wait_send()
-    for i in range(2):
-        far_copy(i).wait_send()
-        far_share(i, core).wait_send()
-    for i in range(n_mp - 1):
-        gain_copy(i).wait_send()
-        lr_copy(i, me_x).wait_send()
-        for j in range(per_x):
-            w2_share(i, j, core).wait_send()
-
-    def drain_w2(bz, _):
-        @pl.when(bz // per_x != me_x)
-        def _():
-            w2_copy(bz).wait_send()
-
-        return 0
-
-    lax.fori_loop(0, n_z, drain_w2, 0)
-
-    def wait_gl(bz, _):
-        for i in range(n_mp - 1):
-            gl_copy(i, bz).wait_send()
-            gl_copy(i, bz).wait_recv()
-        return 0
-
-    lax.fori_loop(0, n_z, wait_gl, 0)
+    thirds = 2 * (n_z - 1)
+    sends = [
+        (wd.at[pl.ds(0, thirds * down_rows // 3), :], z_send.at[0]),
+        (wu.at[pl.ds(0, thirds * rows3), :], z_send.at[1]),
+        (wd.at[pl.ds(0, (n_z - 1) * down_rows // 3), :], y_send.at[0]),
+        (wu.at[pl.ds(0, (n_z - 2) * rows3), :], y_send.at[1]),
+        (wd.at[pl.ds(0, n_z * down_rows), :], c_send.at[0]),
+        (wu.at[pl.ds(0, n_z * up_rows), :], c_send.at[1]),
+        (wu.at[pl.ds(0, rows3), :], far_send.at[0]),
+        (gain_bytes, ga_send.at[0]),
+        (lat_bytes, lr_send.at[0]),
+        (w2_bytes, w2_send.at[0]),
+        (w2_bytes, w2c_send.at[0]),
+        (peer_gl, gl_send.at[0]),
+    ]
+    for ref, sem in sends:
+        remote(ref, ref, sem, c_recv.at[n_z], {"dp": sibling}).wait_send()
+    whole(peer_gl, gl_send, gl_recv).wait_recv()
     inner = jnp.zeros((1, n_tok), F32)
     for b in range(n_mp):
         at = slice(b * lat_cols, (b + 1) * lat_cols)
@@ -507,9 +481,7 @@
     for b in range(n_mp):
         at = slice(b * lat_cols, (b + 1) * lat_cols)
         grad_raw[b] = (own_gl[at, :] / root[...] - lr_t[at, :] * scale).T.astype(BF16)
-    for i in range(n_mp - 1):
-        for j in range(per_x):
-            w2_share(i, j, 1 - core).wait_recv()
+    whole(w2_bytes, w2c_send, w2c_recv).wait_recv()
 
     for k in range(7):
         at = slice(k * r_size, (k + 1) * r_size)
@@ -596,24 +568,22 @@
             pltpu.VMEM((1, n_tok), F32),
             dma((6,)),
             dma((2,)),
-            dma((2, 2, 3, n_z)),
+            dma((2,)),
             dma((2, 3, n_z)),
-            dma((2, n_z)),
-            dma((2, n_z)),
-            dma((2, n_z)),
-            dma((peers,)),
-            dma((peers,)),
-            dma((peers,)),
-            dma((peers,)),
-            dma((n_z,)),
-            dma((peers, n_z // n_mp)),
-            dma((peers, n_z // n_mp)),
-            dma((peers, n_z // n_mp)),
-            dma((peers, n_z)),
-            dma((peers, n_z)),
             dma((2,)),
             dma((2,)),
-            dma((2,)),
+            dma((n_z + 1,)),
+            dma((1,)),
+            dma((1,)),
+            dma((1,)),
+            dma((1,)),
+            dma((1,)),
+            dma((1,)),
+            dma((1,)),
+            dma((1,)),
+            dma((1,)),
+            dma((1,)),
+            dma((1,)),
             pltpu.VMEM(gain.shape, F32),
             pltpu.SMEM(head_counts.shape, jnp.int32),
         ],

time: 137 us -> 132 us (0.964)
  Pallas kernels: 136 us -> 131 us
    pallas_call x1, Pallas kernels: 134 us -> 129 us  [body(): pl.pallas_call(kernel, out_shape=(jax.ShapeDtypeStruct((n_tok, cols), BF1...]
where the time goes in v4:
time: 132 us
  Pallas kernels  131 us (99%)
    pallas_call x1, Pallas kernels, body(): pl.pallas_call(kernel, out_shape=(jax.ShapeDtypeStruct((n_tok, cols), BF1...  129 us

profile of v4, /device:TPU:33, one launch (start us, length us, event | category | flops | bytes accessed | tf_op | source)
XLA Modules:
  0.0 131.9 jit_solution(11611727153363848388)
XLA Ops:
  0.6 128.9 %gather_and_project.1 = (bf16[128,6528]{1,0:T(8,128)(2,1)}, bf16[128,1792]{1,0:T(8,128)(2,1)}) custom-call(bf16[128,7168]{1,0:T(8,128)(2,1)} %tok_h.1, bf16[224,384]{1,0:T(8,128)(2,1)} %wd_h.1, f32[384]{0:T(512)} %gain_h.1, bf16[48,6528]{1,0:T(8,128)(2,1)} %wu_h.1, s32[4]{0:T(128)} %heads_h.1, bf16[128,6528]{1,0:T(8,128)(2,1)} %cot_h.1), custom_call_target="tpu_custom_call" | custom-call | tf_op jit(solution)/shard_map/gather_and_project/pallas_call | solution.py:535
  129.5 2.4 %write_outputs.1 = (bf16[128,6528]{1,0:T(8,128)(2,1)}, bf16[128,1792]{1,0:T(8,128)(2,1)}) custom-call(bf16[128,6528]{1,0:T(8,128)(2,1)} %get-tuple-element.4.q_in, bf16[128,1792]{1,0:T(8,128)(2,1)} %get-tuple-element.5.gt_in), custom_call_target="tpu_custom_call" | custom-call | tf_op jit(solution)/shard_map/write_outputs/pallas_call | solution.py:595

commit v5 on v4

--- a/solution.py
+++ b/solution.py
@@ -194,7 +194,7 @@
         c_copy(kind, bz, 1 - core).wait_recv()
 
     n_lane_tiles = cols // 128
-    cut = n_lane_tiles * 2 // 3 * 128
+    cut = n_lane_tiles * 3 // 4 * 128
 
     def far_part(bz):
         return pl.ds(pl.multiple_of((2 * bz + core) * up_rows + part_c * rows3, rows3), rows3)
@@ -438,13 +438,13 @@
     z_copy(1, 0, far, part_a).wait_recv()
     z_copy(1, 1, far, part_b).wait_recv()
     c_part(far, 0).start()
-    gl_pair(half - 1)
     q_pair(5)
     z_copy(1, 0, far, part_c).wait_recv()
     c_part(far, 1).start()
-    q_pair(6)
+    gl_pair(half - 1)
     wait_sibling(1, far)
     compute([far], q=False)
+    q_pair(6)
     q_pair(7)
     compute([far], gl=False, final=True)
     q_store = pltpu.make_async_copy(q_out, q_h, out_sem.at[0])

time: 132 us -> 132 us (level)
  no operation moved by 1% of the time
where the time goes in v5:
time: 132 us
  Pallas kernels  132 us (100%)
    pallas_call x1, Pallas kernels, body(): pl.pallas_call(kernel, out_shape=(jax.ShapeDtypeStruct((n_tok, cols), BF1...  129 us

profile of v5, /device:TPU:33, one launch (start us, length us, event | category | flops | bytes accessed | tf_op | source)
XLA Modules:
  0.0 132.2 jit_solution(13893683107835673696)
XLA Ops:
  0.6 129.2 %gather_and_project.1 = (bf16[128,6528]{1,0:T(8,128)(2,1)}, bf16[128,1792]{1,0:T(8,128)(2,1)}) custom-call(bf16[128,7168]{1,0:T(8,128)(2,1)} %tok_h.1, bf16[224,384]{1,0:T(8,128)(2,1)} %wd_h.1, f32[384]{0:T(512)} %gain_h.1, bf16[48,6528]{1,0:T(8,128)(2,1)} %wu_h.1, s32[4]{0:T(128)} %heads_h.1, bf16[128,6528]{1,0:T(8,128)(2,1)} %cot_h.1), custom_call_target="tpu_custom_call" | custom-call | tf_op jit(solution)/shard_map/gather_and_project/pallas_call | solution.py:535
  129.8 2.4 %write_outputs.1 = (bf16[128,6528]{1,0:T(8,128)(2,1)}, bf16[128,1792]{1,0:T(8,128)(2,1)}) custom-call(bf16[128,6528]{1,0:T(8,128)(2,1)} %get-tuple-element.4.q_in, bf16[128,1792]{1,0:T(8,128)(2,1)} %get-tuple-element.5.gt_in), custom_call_target="tpu_custom_call" | custom-call | tf_op jit(solution)/shard_map/write_outputs/pallas_call | solution.py:595

commit v6 on v5

--- a/solution.py
+++ b/solution.py
@@ -483,6 +483,12 @@
         grad_raw[b] = (own_gl[at, :] / root[...] - lr_t[at, :] * scale).T.astype(BF16)
     whole(w2_bytes, w2c_send, w2c_recv).wait_recv()
 
+    split = 4 * r_size
+
+    def gt_store(k):
+        at = (slice(0, split), slice(split, out_cols))[k]
+        return pltpu.make_async_copy(gt_out.at[:, at], gt_h.at[:, at], out_sem.at[1 + k])
+
     for k in range(7):
         at = slice(k * r_size, (k + 1) * r_size)
         total = jnp.zeros((n_tok, r_size), F32)
@@ -491,17 +497,19 @@
                 grad_raw[b], wd2[b, at, :], (((1,), (1,)), ((), ())), preferred_element_type=F32
             )
         gt_out[:, at] = total.astype(BF16)
-    gt_store = pltpu.make_async_copy(gt_out, gt_h, out_sem.at[1])
-    gt_store.start()
+        if k == 3:
+            gt_store(0).start()
+    gt_store(1).start()
 
     q_store.wait()
-    gt_store.wait()
+    gt_store(0).wait()
+    gt_store(1).wait()
 
 
 def write_kernel(q_in, gt_in, q_h, gt_h, q_hold, gt_hold, in_sem, out_sem):
     n_tok = q_in.shape[0]
-    quarter = n_tok // 4
-    pairs = [(q_in, q_hold, q_h, slice(k * quarter, (k + 1) * quarter)) for k in range(4)]
+    size = n_tok // 8
+    pairs = [(q_in, q_hold, q_h, slice(k * size, (k + 1) * size)) for k in range(8)]
     pairs.append((gt_in, gt_hold, gt_h, slice(0, n_tok)))
 
     def load(k):
@@ -567,7 +575,7 @@
             pltpu.VMEM((n_tok, out_cols), BF16),
             pltpu.VMEM((1, n_tok), F32),
             dma((6,)),
-            dma((2,)),
+            dma((3,)),
             dma((2,)),
             dma((2, 3, n_z)),
             dma((2,)),
@@ -603,8 +611,8 @@
         scratch_shapes=[
             pltpu.VMEM((n_tok, cols), BF16),
             pltpu.VMEM((n_tok, out_cols), BF16),
-            dma((5,)),
-            dma((5,)),
+            dma((9,)),
+            dma((9,)),
         ],
         name="write_outputs",
     )(queries, grad_tokens)

time: 132 us -> 132 us (level)
  no operation moved by 1% of the time
where the time goes in v6:
time: 132 us
  Pallas kernels  132 us (100%)
    pallas_call x1, Pallas kernels, body(): pl.pallas_call(kernel, out_shape=(jax.ShapeDtypeStruct((n_tok, cols), BF1...  129 us

profile of v6, /device:TPU:33, one launch (start us, length us, event | category | flops | bytes accessed | tf_op | source)
XLA Modules:
  0.0 132.3 jit_solution(17187841781005737116)
XLA Ops:
  0.6 129.1 %gather_and_project.1 = (bf16[128,6528]{1,0:T(8,128)(2,1)}, bf16[128,1792]{1,0:T(8,128)(2,1)}) custom-call(bf16[128,7168]{1,0:T(8,128)(2,1)} %tok_h.1, bf16[224,384]{1,0:T(8,128)(2,1)} %wd_h.1, f32[384]{0:T(512)} %gain_h.1, bf16[48,6528]{1,0:T(8,128)(2,1)} %wu_h.1, s32[4]{0:T(128)} %heads_h.1, bf16[128,6528]{1,0:T(8,128)(2,1)} %cot_h.1), custom_call_target="tpu_custom_call" | custom-call | tf_op jit(solution)/shard_map/gather_and_project/pallas_call | solution.py:543
  129.7 2.6 %write_outputs.1 = (bf16[128,6528]{1,0:T(8,128)(2,1)}, bf16[128,1792]{1,0:T(8,128)(2,1)}) custom-call(bf16[128,6528]{1,0:T(8,128)(2,1)} %get-tuple-element.4.q_in, bf16[128,1792]{1,0:T(8,128)(2,1)} %get-tuple-element.5.gt_in), custom_call_target="tpu_custom_call" | custom-call | tf_op jit(solution)/shard_map/write_outputs/pallas_call | solution.py:603
